TPU v7x, 256 devices: a whole 4x4x8 slice. The times are simulated.
256 devices in a mesh: samp: 8 (over z), seq: 32 (over x, y, core).
Axes of the slice: x: 4, y: 4, z: 8, core: 2. Of those that a mesh axis runs over, the one named last changes fastest.
Arguments:
- queries: bfloat16 [8, 16384, 3584], P('samp', 'seq'), may hold values from -200 to 200
- keys: bfloat16 [8, 16384, 512], P('samp', 'seq'), may hold values from -6 to 6
- values: bfloat16 [8, 16384, 512], P('samp', 'seq'), may hold values from -6 to 6
- reg_owner: int32 [8], P('samp'), may hold values from 0 to 31
- block_lists: int32 [8, 128, 8], P('samp', 'seq'), may hold values from 0 to 127, as said below
- list_counts: int32 [8, 128], P('samp', 'seq'), may hold values from 0 to 8, as said below
- image_blocks: int32 [8, 128], P('samp', 'seq'), may hold values from 0 to 1, as said below
Outputs:
- attended: bfloat16 [8, 16384, 3584], P('samp', 'seq')
Inputs may be any that keep to these rules, and one draw needn't show every extreme that they name: `block_lists`: block b lies on sequence index b // 4. Entry t of a list is used only where t < the block's count, unused entries are 0. The used entries of one block name blocks of distinct sequence indices other than its own. Over all blocks of one sequence index, at most one distinct block of each other sequence index is named. On the last sequence index of each sample, the lists together name a block of every other index. `list_counts`: 0 for image blocks; at most 8. `image_blocks`: the blocks of the last sequence index of each sample are text blocks.
All inputs are finite; a program needn't handle non-finite values.
Results may differ from a plain program's by a relative error of at most 0.0043.
Values may be sent and summed in bfloat16 or wider, within the bound.
A program may use at most 128 MiB of HBM per device.

v0:
```python
import math

import jax
import jax.numpy as jnp
from jax import lax
from jax.sharding import PartitionSpec as P

QUERY_HEADS = 28
KEY_VALUE_HEADS = 4
HEAD_SIZE = 128
REG = 64


very_low = -1e30


def from_root(array, axis, root):
    return lax.dynamic_index_in_dim(lax.all_gather(array, axis), root, 0, keepdims=False)


def joined_along(tiles, dim):
    lengths = list(tiles.shape[1:])
    lengths[dim] *= tiles.shape[0]
    return jnp.moveaxis(tiles, 0, dim).reshape(lengths)


def gather_together(arrays, axis, dims):
    flat = jnp.concatenate([a.reshape(-1) for a in arrays])
    lines, at, done = (lax.all_gather(flat, axis), 0, [])
    for a, dim in zip(arrays, dims):
        tiles = lines[:, at : at + a.size].reshape(-1, *a.shape)
        done.append(joined_along(tiles, dim))
        at += a.size
    return tuple(done)


def group_part(query_row_list, key_row_list, value_row_list, visible):
    head_grouped = query_row_list.reshape(
        query_row_list.shape[0], KEY_VALUE_HEADS, QUERY_HEADS // KEY_VALUE_HEADS, HEAD_SIZE
    )
    per_head_keys = key_row_list.reshape(-1, KEY_VALUE_HEADS, HEAD_SIZE)
    per_head_values = value_row_list.reshape(-1, KEY_VALUE_HEADS, HEAD_SIZE)
    scores = jnp.einsum(
        "qhgd,khd->hgqk", head_grouped, per_head_keys, preferred_element_type=jnp.float32
    ) / math.sqrt(HEAD_SIZE)
    scores = jnp.where(visible, scores, very_low)
    maxima = jnp.max(scores, axis=-1)
    weights = jnp.where(visible, jnp.exp(scores - maxima[..., None]), 0.0)
    totals = jnp.sum(weights, axis=-1)
    partial_value = jnp.einsum(
        "hgqk,khd->hgqd",
        weights.astype(jnp.bfloat16),
        per_head_values,
        preferred_element_type=jnp.float32,
    )
    return (maxima, totals, partial_value)


def combine(parts):
    top_score = jnp.maximum(jnp.maximum(parts[0][0], parts[1][0]), parts[2][0])
    numerator = jnp.zeros(parts[0][2].shape, jnp.float32)
    denominator = jnp.zeros(parts[0][1].shape, jnp.float32)
    for maxima, totals, partial_value in parts:
        rescale = jnp.exp(maxima - top_score)
        numerator = numerator + rescale[..., None] * partial_value
        denominator = denominator + rescale * totals
    merged = numerator / denominator[..., None]
    return merged.transpose(2, 0, 1, 3).reshape(merged.shape[2], -1)


def per_device(queries, keys, values, reg_owner, block_lists, list_counts, image_blocks):
    query_all = queries[0]
    every_key = keys[0]
    every_value = values[0]
    local_lists = block_lists[0]
    local_counts = list_counts[0]
    local_image = image_blocks[0]
    devices = lax.axis_size("seq")
    position = lax.axis_index("seq")
    blocks_here = local_lists.shape[0]
    slot_count = local_lists.shape[1]
    rows_block = every_key.shape[0] // blocks_here
    kv_width = every_key.shape[1]
    stacked = jnp.stack([every_key[:REG], every_value[:REG]])
    registers = from_root(stacked, "seq", reg_owner[0])
    reg_keys = registers[0]
    reg_values = registers[1]
    all_lists, all_counts = gather_together((local_lists, local_counts), "seq", (0, 0))
    own_ids = position * blocks_here + jnp.arange(blocks_here, dtype=jnp.int32)
    live_slots = jnp.arange(slot_count, dtype=jnp.int32)[None, :] < all_counts[:, None]
    named_here = (all_lists[:, :, None] == own_ids[None, None, :]) & live_slots[:, :, None]
    wanted = jnp.any(named_here, axis=1).reshape(devices, blocks_here, blocks_here)
    selector = jnp.any(wanted, axis=1).astype(jnp.bfloat16)
    send_keys = jnp.dot(
        selector,
        every_key.reshape(blocks_here, rows_block * kv_width),
        preferred_element_type=jnp.float32,
    ).astype(jnp.bfloat16)
    send_values = jnp.dot(
        selector,
        every_value.reshape(blocks_here, rows_block * kv_width),
        preferred_element_type=jnp.float32,
    ).astype(jnp.bfloat16)
    owners = (local_lists // blocks_here).reshape(-1)
    got_keys, got_values = (
        lax.all_to_all(
            send_keys.reshape(devices, rows_block, kv_width),
            "seq",
            split_axis=0,
            concat_axis=0,
            tiled=True,
        ),
        lax.all_to_all(
            send_values.reshape(devices, rows_block, kv_width),
            "seq",
            split_axis=0,
            concat_axis=0,
            tiled=True,
        ),
    )
    remote_keys = got_keys[owners]
    remote_values = got_values[owners]
    remote_keys = remote_keys.reshape(blocks_here, slot_count * rows_block, kv_width)
    remote_values = remote_values.reshape(blocks_here, slot_count * rows_block, kv_width)
    row_ids = jnp.arange(rows_block)
    slot_rows = jnp.arange(slot_count * rows_block) // rows_block

    def attend(pieces):
        query_row_list, own_keys, own_values, named_keys, named_values, list_count, is_image = (
            pieces
        )
        reg_visible = jnp.ones((rows_block, reg_keys.shape[0]), bool)
        own_visible = (row_ids[None, :] <= row_ids[:, None]) | (is_image == 1)
        far_visible = jnp.broadcast_to(
            slot_rows[None, :] < list_count, (rows_block, slot_count * rows_block)
        )
        parts = [
            group_part(query_row_list, reg_keys, reg_values, reg_visible),
            group_part(query_row_list, own_keys, own_values, own_visible),
            group_part(query_row_list, named_keys, named_values, far_visible),
        ]
        return combine(parts).astype(jnp.bfloat16)

    blocks_out = lax.map(
        attend,
        (
            query_all.reshape(blocks_here, rows_block, -1),
            every_key.reshape(blocks_here, rows_block, kv_width),
            every_value.reshape(blocks_here, rows_block, kv_width),
            remote_keys,
            remote_values,
            local_counts,
            local_image,
        ),
    )
    return blocks_out.reshape(1, blocks_here * rows_block, -1)


def solution(mesh):
    placed = (
        P("samp", "seq", None),
        P("samp", "seq", None),
        P("samp", "seq", None),
        P("samp"),
        P("samp", "seq", None),
        P("samp", "seq"),
        P("samp", "seq"),
    )
    return jax.shard_map(
        per_device, mesh=mesh, in_specs=placed, out_specs=P("samp", "seq", None), check_vma=False
    )
```

profile of v0, /device:TPU:1, one launch (start us, length us, event | category | flops | bytes accessed | tf_op | source)
XLA Modules:
  0.0 332.7 jit_solution(4831803068312926073)
XLA Ops:
  10.1 14.7 %all-reduce = s32[1152]{0:T(1024)S(1)} all-reduce(s32[1152]{0:T(1024)S(1)} %add_dynamic-update-slice_fusion), channel_id=3, replica_groups=mesh['samp'=8,'seq'=32] {'seq'}, use_global_device_ids=true, to_apply=%add | all-reduce | flops 1152 | bytes 9216
  25.4 1.4 reshape_squeeze.29
  28.3 3.5 %copy.117 = bf16[4,8,128,512]{3,2,1,0:T(8,128)(2,1)} copy(bf16[4,8,128,512]{3,1,2,0:T(8,128)(2,1)S(1)} %bitcast.265) | data formatting | bytes 8388608
  31.8 8.5 %all-to-all-start.1 = ((bf16[32,128,512]{2,1,0:T(8,128)(2,1)}), bf16[32,128,512]{2,1,0:T(8,128)(2,1)}, u32[]{:S(2)}, u32[]{:S(2)}) async-start(bf16[32,128,512]{2,1,0:T(8,128)(2,1)} %bitcast.263), calls=%async_computation.1 | async-start | bytes 8388608 | tf_op jit(solution)/shard_map/all_to_all | solution.py:113
  41.9 1.4 reshape_squeeze.27
  44.7 3.5 %copy.116 = bf16[4,8,128,512]{3,2,1,0:T(8,128)(2,1)} copy(bf16[4,8,128,512]{3,1,2,0:T(8,128)(2,1)S(1)} %bitcast.264) | data formatting | bytes 8388608
  48.2 45.9 %all-to-all-done.1 = bf16[32,128,512]{2,1,0:T(8,128)(2,1)} async-done(((bf16[32,128,512]{2,1,0:T(8,128)(2,1)}), bf16[32,128,512]{2,1,0:T(8,128)(2,1)}, u32[]{:S(2)}, u32[]{:S(2)}) %all-to-all-start.1) | async-done | bytes 4194336 | tf_op jit(solution)/shard_map/all_to_all | solution.py:113
  94.1 7.2 %all-to-all-start = ((bf16[32,128,512]{2,1,0:T(8,128)(2,1)}), bf16[32,128,512]{2,1,0:T(8,128)(2,1)}, u32[]{:S(2)}, u32[]{:S(2)}) async-start(bf16[32,128,512]{2,1,0:T(8,128)(2,1)} %bitcast.262), calls=%async_computation | async-start | bytes 8388608 | tf_op jit(solution)/shard_map/all_to_all | solution.py:106
  102.2 5.3 %gather_fusion.1 = bf16[32,128,512]{2,1,0:T(8,128)(2,1)} fusion(bf16[32,128,512]{2,1,0:T(8,128)(2,1)} %all-to-all-done.1, s32[1024]{0:T(1024)S(1)} %pad_clamp_fusion), kind=kCustom, calls=%fused_computation.1 | custom fusion | bytes 8388736 | tf_op jit(solution)/shard_map/gather | solution.py:122
  107.5 52.8 %all-to-all-done = bf16[32,128,512]{2,1,0:T(8,128)(2,1)} async-done(((bf16[32,128,512]{2,1,0:T(8,128)(2,1)}), bf16[32,128,512]{2,1,0:T(8,128)(2,1)}, u32[]{:S(2)}, u32[]{:S(2)}) %all-to-all-start) | async-done | bytes 4194336 | tf_op jit(solution)/shard_map/all_to_all | solution.py:106
  160.3 5.0 %gather_fusion = bf16[32,128,512]{2,1,0:T(8,128)(2,1)} fusion(bf16[32,128,512]{2,1,0:T(8,128)(2,1)} %all-to-all-done, s32[1024]{0:T(1024)S(1)} %pad_clamp_fusion), kind=kCustom, calls=%fused_computation | custom fusion | bytes 8388736 | tf_op jit(solution)/shard_map/gather | solution.py:121
  166.9 159.0 %while.12 = (s32[]{:T(128)}, bf16[4,128,3584]{2,1,0:T(8,128)(2,1)}, bf16[4,128,3584]{2,1,0:T(8,128)(2,1)}, bf16[1,64,512]{2,1,0:T(8,128)(2,1)}, s32[4]{0:T(128)S...) while((s32[]{:T(128)}, bf16[4,128,3584]{2,1,0:T(8,128)(2,1)}, ...), condition=%wide.wide.region_9.10_spmd.clone, body=%wide.wide.region_2.9_spmd.clone.sunk | while | flops 2289687552 | bytes 158516048 | solution.py:144
  172.1 3.0 constant_dynamic-slice_fusion.13
  175.1 2.3 copy.146
  178.7 4.4 %bitcast_reduce_fusion.3 = (f32[4,7,128]{2,1,0:T(8,128)S(1)}, f32[4,1024,128,7]{2,1,3,0:T(8,128)S(1)}) fusion(pred[1024]{0:T(1024)(128)(4,1)S(1)} %fusion.128, bf16[1024,4,128,1]{0,2,3,1:T(8,128)(2,1)} %bitcast.257, bf16[128,4,7,128]{0,3,2,1:T(8,128)(2,1)S(1)} %bitcast.255), kind=kOutput, calls=%fused_computation.5.clone.clone.1 | convolution fusion | flops 950530560 | bytes 16661504 | tf_op jit(solution)/shard_map/while/body/eval_jaxpr/qhgd,khd->hgqk/dot_general | solution.py:43
  183.1 4.2 %fusion.129 = f32[4,7,128]{2,1,0:T(8,128)S(1)} fusion(f32[4,1024,128,7]{2,1,3,0:T(8,128)S(1)} %get-tuple-element.349, f32[4,7,128]{2,1,0:T(8,128)S(1)} %get-tuple-element.350, pred[1024]{0:T(1024)(128)(4,1)S(1)} %fusion.128), kind=kLoop, calls=%fused_computation.9.clone.clone.1 | loop fusion | flops 18346496 | bytes 14709760 | tf_op jit(solution)/shard_map/while/body/eval_jaxpr/reduce_sum | solution.py:49
  189.9 1.9 fusion.125
  191.8 1.7 fusion.127
  193.5 1.5 copy.145
  195.0 9.1 %fusion.133 = bf16[128,4,7,128]{0,3,2,1:T(8,128)(2,1)} fusion(f32[4,7,128,128]{2,3,1,0:T(8,128)S(1)} %copy-done.3, f32[4,7,128,128]{2,3,1,0:T(8,128)} %fusion.127, bf16[1024,4,128,1]{0,2,3,1:T(8,128)(2,1)S(1)} %bitcast.258, f32[4,1024,128,7]{2,1,3,0:T(8,128)} %copy-done, f32[4,7,128]{2,1,0:T(8,128)S(1)} %get-tuple-element.350, ...), kind=kOutput, calls=%fused_computation.17.clone.clone.1 | convolution fusion | flops 961085440 | bytes 20388864 | tf_op jit(solution)/shard_map/while/body/eval_jaxpr/hgqk,khd->hgqd/dot_general | solution.py:50
  204.1 1.5 copy.147
  211.8 3.0 constant_dynamic-slice_fusion.13
  214.8 2.3 copy.146
  218.4 4.4 %bitcast_reduce_fusion.3 = (f32[4,7,128]{2,1,0:T(8,128)S(1)}, f32[4,1024,128,7]{2,1,3,0:T(8,128)S(1)}) fusion(pred[1024]{0:T(1024)(128)(4,1)S(1)} %fusion.128, bf16[1024,4,128,1]{0,2,3,1:T(8,128)(2,1)} %bitcast.257, bf16[128,4,7,128]{0,3,2,1:T(8,128)(2,1)S(1)} %bitcast.255), kind=kOutput, calls=%fused_computation.5.clone.clone.1 | convolution fusion | flops 950530560 | bytes 16661504 | tf_op jit(solution)/shard_map/while/body/eval_jaxpr/qhgd,khd->hgqk/dot_general | solution.py:43
  222.9 4.2 %fusion.129 = f32[4,7,128]{2,1,0:T(8,128)S(1)} fusion(f32[4,1024,128,7]{2,1,3,0:T(8,128)S(1)} %get-tuple-element.349, f32[4,7,128]{2,1,0:T(8,128)S(1)} %get-tuple-element.350, pred[1024]{0:T(1024)(128)(4,1)S(1)} %fusion.128), kind=kLoop, calls=%fused_computation.9.clone.clone.1 | loop fusion | flops 18346496 | bytes 14709760 | tf_op jit(solution)/shard_map/while/body/eval_jaxpr/reduce_sum | solution.py:49
  229.7 1.9 fusion.125
  231.5 1.7 fusion.127
  233.2 1.5 copy.145
  234.7 9.1 %fusion.133 = bf16[128,4,7,128]{0,3,2,1:T(8,128)(2,1)} fusion(f32[4,7,128,128]{2,3,1,0:T(8,128)S(1)} %copy-done.3, f32[4,7,128,128]{2,3,1,0:T(8,128)} %fusion.127, bf16[1024,4,128,1]{0,2,3,1:T(8,128)(2,1)S(1)} %bitcast.258, f32[4,1024,128,7]{2,1,3,0:T(8,128)} %copy-done, f32[4,7,128]{2,1,0:T(8,128)S(1)} %get-tuple-element.350, ...), kind=kOutput, calls=%fused_computation.17.clone.clone.1 | convolution fusion | flops 961085440 | bytes 20388864 | tf_op jit(solution)/shard_map/while/body/eval_jaxpr/hgqk,khd->hgqd/dot_general | solution.py:50
  243.9 1.5 copy.147
  251.5 3.0 constant_dynamic-slice_fusion.13
  254.6 2.3 copy.146
  258.2 4.4 %bitcast_reduce_fusion.3 = (f32[4,7,128]{2,1,0:T(8,128)S(1)}, f32[4,1024,128,7]{2,1,3,0:T(8,128)S(1)}) fusion(pred[1024]{0:T(1024)(128)(4,1)S(1)} %fusion.128, bf16[1024,4,128,1]{0,2,3,1:T(8,128)(2,1)} %bitcast.257, bf16[128,4,7,128]{0,3,2,1:T(8,128)(2,1)S(1)} %bitcast.255), kind=kOutput, calls=%fused_computation.5.clone.clone.1 | convolution fusion | flops 950530560 | bytes 16661504 | tf_op jit(solution)/shard_map/while/body/eval_jaxpr/qhgd,khd->hgqk/dot_general | solution.py:43
  262.6 4.2 %fusion.129 = f32[4,7,128]{2,1,0:T(8,128)S(1)} fusion(f32[4,1024,128,7]{2,1,3,0:T(8,128)S(1)} %get-tuple-element.349, f32[4,7,128]{2,1,0:T(8,128)S(1)} %get-tuple-element.350, pred[1024]{0:T(1024)(128)(4,1)S(1)} %fusion.128), kind=kLoop, calls=%fused_computation.9.clone.clone.1 | loop fusion | flops 18346496 | bytes 14709760 | tf_op jit(solution)/shard_map/while/body/eval_jaxpr/reduce_sum | solution.py:49
  269.4 1.9 fusion.125
  271.3 1.7 fusion.127
  273.0 1.5 copy.145
  274.5 9.1 %fusion.133 = bf16[128,4,7,128]{0,3,2,1:T(8,128)(2,1)} fusion(f32[4,7,128,128]{2,3,1,0:T(8,128)S(1)} %copy-done.3, f32[4,7,128,128]{2,3,1,0:T(8,128)} %fusion.127, bf16[1024,4,128,1]{0,2,3,1:T(8,128)(2,1)S(1)} %bitcast.258, f32[4,1024,128,7]{2,1,3,0:T(8,128)} %copy-done, f32[4,7,128]{2,1,0:T(8,128)S(1)} %get-tuple-element.350, ...), kind=kOutput, calls=%fused_computation.17.clone.clone.1 | convolution fusion | flops 961085440 | bytes 20388864 | tf_op jit(solution)/shard_map/while/body/eval_jaxpr/hgqk,khd->hgqd/dot_general | solution.py:50
  283.6 1.5 copy.147
  291.3 3.0 constant_dynamic-slice_fusion.13
  294.3 2.3 copy.146
  297.9 4.4 %bitcast_reduce_fusion.3 = (f32[4,7,128]{2,1,0:T(8,128)S(1)}, f32[4,1024,128,7]{2,1,3,0:T(8,128)S(1)}) fusion(pred[1024]{0:T(1024)(128)(4,1)S(1)} %fusion.128, bf16[1024,4,128,1]{0,2,3,1:T(8,128)(2,1)} %bitcast.257, bf16[128,4,7,128]{0,3,2,1:T(8,128)(2,1)S(1)} %bitcast.255), kind=kOutput, calls=%fused_computation.5.clone.clone.1 | convolution fusion | flops 950530560 | bytes 16661504 | tf_op jit(solution)/shard_map/while/body/eval_jaxpr/qhgd,khd->hgqk/dot_general | solution.py:43
  302.3 4.2 %fusion.129 = f32[4,7,128]{2,1,0:T(8,128)S(1)} fusion(f32[4,1024,128,7]{2,1,3,0:T(8,128)S(1)} %get-tuple-element.349, f32[4,7,128]{2,1,0:T(8,128)S(1)} %get-tuple-element.350, pred[1024]{0:T(1024)(128)(4,1)S(1)} %fusion.128), kind=kLoop, calls=%fused_computation.9.clone.clone.1 | loop fusion | flops 18346496 | bytes 14709760 | tf_op jit(solution)/shard_map/while/body/eval_jaxpr/reduce_sum | solution.py:49
  309.1 1.9 fusion.125
  311.0 1.7 fusion.127
  312.7 1.5 copy.145
  314.2 9.1 %fusion.133 = bf16[128,4,7,128]{0,3,2,1:T(8,128)(2,1)} fusion(f32[4,7,128,128]{2,3,1,0:T(8,128)S(1)} %copy-done.3, f32[4,7,128,128]{2,3,1,0:T(8,128)} %fusion.127, bf16[1024,4,128,1]{0,2,3,1:T(8,128)(2,1)S(1)} %bitcast.258, f32[4,1024,128,7]{2,1,3,0:T(8,128)} %copy-done, f32[4,7,128]{2,1,0:T(8,128)S(1)} %get-tuple-element.350, ...), kind=kOutput, calls=%fused_computation.17.clone.clone.1 | convolution fusion | flops 961085440 | bytes 20388864 | tf_op jit(solution)/shard_map/while/body/eval_jaxpr/hgqk,khd->hgqd/dot_general | solution.py:50
  323.3 1.5 copy.147
  (142 shorter events, 46.7 us)
Async XLA Ops:
  31.8 9.4 %slice-start = ((bf16[1,512,512]{2,1,0:T(8,128)(2,1)}), bf16[1,64,512]{2,1,0:T(8,128)(2,1)S(1)}, s32[]{:S(2)}) async-start(bf16[1,512,512]{2,1,0:T(8,128)(2,1)} %param.11), calls=%async_computation.3 | async-start | bytes 131072 | tf_op jit(solution)/shard_map/slice | solution.py:84
  31.8 62.3 %all-to-all-start.1 = ((bf16[32,128,512]{2,1,0:T(8,128)(2,1)}), bf16[32,128,512]{2,1,0:T(8,128)(2,1)}, u32[]{:S(2)}, u32[]{:S(2)}) async-start(bf16[32,128,512]{2,1,0:T(8,128)(2,1)} %bitcast.263), calls=%async_computation.1 | async-start | bytes 8388608 | tf_op jit(solution)/shard_map/all_to_all | solution.py:113
  40.3 125.0 %all-gather.4.cloned.1.call-start = ((), (), s32[]{:S(2)}) async-start(), calls=%async_computation.2 | async-start | bytes 4325376 | tf_op jit(solution)/shard_map/all_gather | solution.py:18
  94.1 7.2 %copy-start.8 = (s32[1,4,8]{2,1,0:T(4,128)S(1)}, s32[1,4,8]{2,1,0:T(4,128)}, u32[]{:S(2)}) copy-start(s32[1,4,8]{2,1,0:T(4,128)} %param.13) | copy-start | bytes 388
  94.1 66.2 %all-to-all-start = ((bf16[32,128,512]{2,1,0:T(8,128)(2,1)}), bf16[32,128,512]{2,1,0:T(8,128)(2,1)}, u32[]{:S(2)}, u32[]{:S(2)}) async-start(bf16[32,128,512]{2,1,0:T(8,128)(2,1)} %bitcast.262), calls=%async_computation | async-start | bytes 8388608 | tf_op jit(solution)/shard_map/all_to_all | solution.py:106
  107.5 59.4 %copy-start.4 = (bf16[1,512,512]{2,1,0:T(8,128)(2,1)S(1)}, bf16[1,512,512]{2,1,0:T(8,128)(2,1)}, u32[]{:S(2)}) copy-start(bf16[1,512,512]{2,1,0:T(8,128)(2,1)} %param.11) | copy-start | bytes 1572868
  107.5 59.4 %copy-start.9 = (s32[1,4]{1,0:T(1,128)S(1)}, s32[1,4]{1,0:T(1,128)}, u32[]{:S(2)}) copy-start(s32[1,4]{1,0:T(1,128)} %param.14) | copy-start | bytes 52
  107.5 59.4 %copy-start.10 = (s32[1,4]{1,0:T(1,128)S(1)}, s32[1,4]{1,0:T(1,128)}, u32[]{:S(2)}) copy-start(s32[1,4]{1,0:T(1,128)} %param.15) | copy-start | bytes 52
  166.2 0.6 copy-start.6
  166.2 0.7 copy-start.7
  183.1 5.2 %copy-start = (f32[4,1024,128,7]{2,1,3,0:T(8,128)}, f32[4,1024,128,7]{2,1,3,0:T(8,128)S(1)}, u32[]{:S(2)}) copy-start(f32[4,1024,128,7]{2,1,3,0:T(8,128)S(1)} %get-tuple-element.349) | copy-start | bytes 44040196 | tf_op jit(solution)/shard_map/while
  188.6 0.9 copy-start.1
  189.8 2.0 copy-start.2
  191.8 3.2 copy-start.3
  204.1 2.5 copy-start.5
  222.9 5.2 %copy-start = (f32[4,1024,128,7]{2,1,3,0:T(8,128)}, f32[4,1024,128,7]{2,1,3,0:T(8,128)S(1)}, u32[]{:S(2)}) copy-start(f32[4,1024,128,7]{2,1,3,0:T(8,128)S(1)} %get-tuple-element.349) | copy-start | bytes 44040196 | tf_op jit(solution)/shard_map/while
  228.4 0.9 copy-start.1
  229.5 2.0 copy-start.2
  231.5 3.2 copy-start.3
  243.9 2.5 copy-start.5
  262.6 5.2 %copy-start = (f32[4,1024,128,7]{2,1,3,0:T(8,128)}, f32[4,1024,128,7]{2,1,3,0:T(8,128)S(1)}, u32[]{:S(2)}) copy-start(f32[4,1024,128,7]{2,1,3,0:T(8,128)S(1)} %get-tuple-element.349) | copy-start | bytes 44040196 | tf_op jit(solution)/shard_map/while
  268.1 0.9 copy-start.1
  269.2 2.0 copy-start.2
  271.3 3.2 copy-start.3
  283.6 2.5 copy-start.5
  302.3 5.2 %copy-start = (f32[4,1024,128,7]{2,1,3,0:T(8,128)}, f32[4,1024,128,7]{2,1,3,0:T(8,128)S(1)}, u32[]{:S(2)}) copy-start(f32[4,1024,128,7]{2,1,3,0:T(8,128)S(1)} %get-tuple-element.349) | copy-start | bytes 44040196 | tf_op jit(solution)/shard_map/while
  307.9 0.9 copy-start.1
  309.0 2.0 copy-start.2
  311.0 3.2 copy-start.3
  323.3 2.5 copy-start.5
Sparse Core Ops, SparseCore 0:
  43.7 113.6 all-gather.3
where the time goes:
time: 334 us; the launch traced here: 333 us
  waiting for transfers between devices  98.8 us (30%)
  local copies, waits for them, and re-layouts  87.1 us (26%)
  matrix products  74.1 us (22%)
  other arithmetic  24.2 us (7%)
  starting transfers between devices  15.8 us (5%)
  between operations  14.9 us (4%)
  blocking collectives  14.7 us (4%)
    all_to_all x1, waiting for transfers between devices, per_device(): lax.all_to_all(send_keys.reshape(devices, rows_block, kv_width), 'seq', s...  52.8 us
    dot_general x12, matrix products, group_part(): jnp.einsum('hgqk,khd->hgqd', weights.astype(jnp.bfloat16), per_head_value...  50.8 us
    all_to_all x1, waiting for transfers between devices, per_device(): lax.all_to_all(send_values.reshape(devices, rows_block, kv_width), 'seq',...  45.9 us
    dynamic_slice x40, local copies, waits for them, and re-layouts, per_device(): lax.map(attend, (query_all.reshape(blocks_here, rows_block, -1), every_ke...  44.3 us
    dot_general x12, matrix products, group_part(): jnp.einsum('qhgd,khd->hgqk', head_grouped, per_head_keys, preferred_eleme...  20.7 us
    reduce_sum x12, other arithmetic, group_part(): totals = jnp.sum(weights, axis=-1)  19.6 us
    unnamed x1, blocking collectives  14.7 us
    dynamic_update_slice x8, local copies, waits for them, and re-layouts, per_device(): lax.map(attend, (query_all.reshape(blocks_here, rows_block, -1), every_ke...  9.99 us
  transfers between devices with their start and end apart: 3, of which 2 were waited for; matrix products, arithmetic and copies ran while one was open for 5% of the time, Pallas kernels for 0%

commit v1 on v0

v1 whole, which is shorter than its diff:
```python
import math

import jax
import jax.numpy as jnp
from jax import lax
from jax.experimental import pallas as pl
from jax.experimental.pallas import tpu as pltpu
from jax.sharding import PartitionSpec as P

QUERY_HEADS = 28
KEY_VALUE_HEADS = 4
HEAD_SIZE = 128
REG = 64
GROUP = QUERY_HEADS // KEY_VALUE_HEADS
SCALE = math.log2(math.e) / math.sqrt(HEAD_SIZE)


very_low = -1e30


def from_root(array, axis, root):
    return lax.dynamic_index_in_dim(lax.all_gather(array, axis), root, 0, keepdims=False)


def gather_together(arrays, axis):
    flat = jnp.concatenate([a.reshape(-1) for a in arrays])
    lines, at, done = (lax.all_gather(flat, axis), 0, [])
    for a in arrays:
        tiles = lines[:, at : at + a.size].reshape(-1, *a.shape[1:])
        done.append(tiles)
        at += a.size
    return tuple(done)


def dot_t(a, b):
    return lax.dot_general(a, b, (((1,), (1,)), ((), ())), preferred_element_type=jnp.float32)


def attend(q, reg_k, reg_v, own_k, own_v, far, is_image):
    rows = q.shape[0]
    stacked = jnp.concatenate(
        [q[:, g * HEAD_SIZE : (g + 1) * HEAD_SIZE] for g in range(GROUP)], axis=0
    )
    reg_keys = jnp.concatenate([reg_k, reg_k], axis=0)
    zero = jnp.zeros((rows, HEAD_SIZE), jnp.bfloat16)
    ones = jnp.ones((rows, HEAD_SIZE), jnp.bfloat16)
    half = jnp.concatenate([ones[:REG], zero[:REG]], axis=0)
    reg_values = jnp.concatenate([reg_v, zero[:REG]], axis=0)
    slots = [(own_k, own_v, ones), (reg_keys, reg_values, half)]
    for k, v, used in far:
        slots.append(
            (jnp.where(used, k, reg_keys), jnp.where(used, v, zero), jnp.where(used, ones, zero))
        )
    visible = (
        lax.broadcasted_iota(jnp.int32, (rows, rows), 1)
        <= lax.broadcasted_iota(jnp.int32, (rows, rows), 0)
    ) | is_image
    seen = jnp.concatenate([visible] * GROUP, axis=0)
    scores = []
    for i in range(0, len(slots), 2):
        scores.append(dot_t(stacked, jnp.concatenate([slots[i][0], slots[i + 1][0]], axis=0)))
    scores[0] = jnp.concatenate(
        [jnp.where(seen, scores[0][:, :rows], very_low), scores[0][:, rows:]], axis=1
    )
    top = scores[0]
    for s in scores[1:]:
        top = jnp.maximum(top, s)
    top = jnp.max(top, axis=1, keepdims=True)
    total = None
    for i, s in enumerate(scores):
        weights = jnp.exp2((s - top) * SCALE).astype(jnp.bfloat16)
        a, b = slots[2 * i], slots[2 * i + 1]
        rhs = jnp.concatenate(
            [jnp.concatenate([a[1], a[2]], axis=1), jnp.concatenate([b[1], b[2]], axis=1)], axis=0
        )
        part = jnp.dot(weights, rhs, preferred_element_type=jnp.float32)
        total = part if total is None else total + part
    merged = (total[:, :HEAD_SIZE] / total[:, HEAD_SIZE:]).astype(jnp.bfloat16)
    return jnp.concatenate([merged[g * rows : (g + 1) * rows] for g in range(GROUP)], axis=1)


def attention_kernel(
    place, counts, image, q_ref, k_ref, v_ref, reg_ref, far_k_ref, far_v_ref, out_ref
):
    b = pl.program_id(1)
    far = []
    for t in range(8):
        j = place[b, t]
        far.append((far_k_ref[j], far_v_ref[j], t < counts[b]))
    out_ref[...] = attend(
        q_ref[...], reg_ref[0], reg_ref[1], k_ref[...], v_ref[...], far, image[b] == 1
    )


def attention(q, k, v, registers, far_k, far_v, place, counts, image):
    blocks = place.shape[0]
    rows = q.shape[0] // blocks
    width = GROUP * HEAD_SIZE
    devices = far_k.shape[0]
    return pl.pallas_call(
        attention_kernel,
        out_shape=jax.ShapeDtypeStruct(q.shape, jnp.bfloat16),
        grid_spec=pltpu.PrefetchScalarGridSpec(
            num_scalar_prefetch=3,
            grid=(KEY_VALUE_HEADS, blocks),
            in_specs=[
                pl.BlockSpec((rows, width), lambda h, b, *_: (b, h)),
                pl.BlockSpec((rows, HEAD_SIZE), lambda h, b, *_: (b, h)),
                pl.BlockSpec((rows, HEAD_SIZE), lambda h, b, *_: (b, h)),
                pl.BlockSpec((2, REG, HEAD_SIZE), lambda h, b, *_: (0, 0, h)),
                pl.BlockSpec((devices, rows, HEAD_SIZE), lambda h, b, *_: (0, 0, h)),
                pl.BlockSpec((devices, rows, HEAD_SIZE), lambda h, b, *_: (0, 0, h)),
            ],
            out_specs=pl.BlockSpec((rows, width), lambda h, b, *_: (b, h)),
        ),
        compiler_params=pltpu.CompilerParams(vmem_limit_bytes=56 << 20),
        name="attention",
    )(place, counts, image, q, k, v, registers, far_k, far_v)


def per_device(queries, keys, values, reg_owner, block_lists, list_counts, image_blocks):
    every_key = keys[0]
    every_value = values[0]
    local_lists = block_lists[0]
    local_counts = list_counts[0]
    devices = lax.axis_size("seq")
    position = lax.axis_index("seq")
    blocks_here = local_lists.shape[0]
    slot_count = local_lists.shape[1]
    rows_block = every_key.shape[0] // blocks_here
    kv_width = every_key.shape[1]
    stacked = jnp.stack([every_key[:REG], every_value[:REG]])
    registers = from_root(stacked, "seq", reg_owner[0])
    all_lists, all_counts = gather_together((local_lists, local_counts), "seq")
    own_ids = position * blocks_here + jnp.arange(blocks_here, dtype=jnp.int32)
    live_slots = jnp.arange(slot_count, dtype=jnp.int32)[None, :] < all_counts[:, None]
    named_here = (all_lists[:, :, None] == own_ids[None, None, :]) & live_slots[:, :, None]
    wanted = jnp.any(named_here, axis=1).reshape(devices, blocks_here, blocks_here)
    selector = jnp.any(wanted, axis=1).astype(jnp.bfloat16)
    exchanged = []
    for array in (every_key, every_value):
        sent = jnp.dot(
            selector,
            array.reshape(blocks_here, rows_block * kv_width),
            preferred_element_type=jnp.float32,
        ).astype(jnp.bfloat16)
        exchanged.append(
            lax.all_to_all(
                sent.reshape(devices, rows_block, kv_width),
                "seq",
                split_axis=0,
                concat_axis=0,
                tiled=True,
            )
        )
    out = attention(
        queries[0],
        every_key,
        every_value,
        registers,
        exchanged[0],
        exchanged[1],
        local_lists // blocks_here,
        local_counts,
        image_blocks[0],
    )
    return out[None]


def solution(mesh):
    placed = (
        P("samp", "seq", None),
        P("samp", "seq", None),
        P("samp", "seq", None),
        P("samp"),
        P("samp", "seq", None),
        P("samp", "seq"),
        P("samp", "seq"),
    )
    return jax.shard_map(
        per_device, mesh=mesh, in_specs=placed, out_specs=P("samp", "seq", None), check_vma=False
    )
```

time: 334 us -> 212 us (0.63)
  local copies, waits for them, and re-layouts: 87.1 us -> 14.6 us
  matrix products: 74.1 us -> 2.64 us
  Pallas kernels: 0 us -> 44.4 us
  other arithmetic: 24.2 us -> 2.36 us
  waiting for transfers between devices: 98.8 us -> 103 us
    dot_general x26 -> x2, matrix products: 74.1 us -> 2.64 us  [per_device(): jnp.dot(selector, array.reshape(blocks_here, rows_block * kv_width), pref...]
    pallas_call x0 -> x1, Pallas kernels: none -> 44.4 us  [attention(): pl.pallas_call(attention_kernel, out_shape=jax.ShapeDtypeStruct(q.shape,...]
    dynamic_slice x40 -> x0, local copies, waits for them, and re-layouts: 44.3 us -> none  [per_device(): lax.map(attend, (query_all.reshape(blocks_here, rows_block, -1), every_ke...]
    reduce_sum x12 -> x0, other arithmetic: 19.6 us -> none  [group_part(): totals = jnp.sum(weights, axis=-1)]
    gather x2 -> x0, local copies, waits for them, and re-layouts: 10.3 us -> none  [the longest x1 5.31 us: per_device(): remote_values = got_values[owners]]
    dynamic_update_slice x8 -> x0, local copies, waits for them, and re-layouts: 9.99 us -> none  [per_device(): lax.map(attend, (query_all.reshape(blocks_here, rows_block, -1), every_ke...]
    while x40 -> x0, local copies, waits for them, and re-layouts: 7.58 us -> none
    all_to_all x2, waiting for transfers between devices: 98.7 us -> 103 us  [per_device(): lax.all_to_all(sent.reshape(devices, rows_block, kv_width), 'seq', split_...]
  transfers between devices with their start and end apart: 3 -> 3, of which waited for: 2 -> 2; matrix products, arithmetic and copies ran while one was open for 5% -> 8% of each run, Pallas kernels for 0% -> 0%
where the time goes in v1:
time: 212 us; the launch traced here: 211 us
  waiting for transfers between devices  103 us (49%)
  Pallas kernels  44.4 us (21%)
  blocking collectives  14.7 us (7%)
  between operations  14.7 us (7%)
  local copies, waits for them, and re-layouts  14.6 us (7%)
  starting transfers between devices  14.3 us (7%)
  matrix products  2.64 us (1%)
  other arithmetic  2.36 us (1%)
    all_to_all x2, waiting for transfers between devices, per_device(): lax.all_to_all(sent.reshape(devices, rows_block, kv_width), 'seq', split_...  103 us
    pallas_call x1, Pallas kernels, attention(): pl.pallas_call(attention_kernel, out_shape=jax.ShapeDtypeStruct(q.shape,...  44.4 us
    unnamed x1, blocking collectives  14.7 us
    all_to_all x2, starting transfers between devices, per_device(): lax.all_to_all(sent.reshape(devices, rows_block, kv_width), 'seq', split_...  14.3 us
    unnamed x8, local copies, waits for them, and re-layouts  8.24 us
  transfers between devices with their start and end apart: 3, of which 2 were waited for; matrix products, arithmetic and copies ran while one was open for 8% of the time, Pallas kernels for 0%

profile of v1, /device:TPU:1, one launch (start us, length us, event | category | flops | bytes accessed | tf_op | source)
XLA Modules:
  0.0 211.0 jit_solution(9977866505138561095)
XLA Ops:
  6.5 0.0 all-gather.4.cloned.1.call-start
  6.5 0.8 slice.14
  7.4 0.8 slice.15
  8.2 0.7 pad_maximum_fusion
  8.9 0.0 all-gather.4.cloned.1.call-update
  8.9 1.4 reshape_squeeze.10
  10.4 0.8 reshape_squeeze.9
  11.1 1.3 dynamic-slice
  13.0 0.8 add_dynamic-update-slice_fusion
  13.9 14.7 %all-reduce = s32[1152]{0:T(1024)S(1)} all-reduce(s32[1152]{0:T(1024)S(1)} %add_dynamic-update-slice_fusion), channel_id=3, replica_groups=mesh['samp'=8,'seq'=32] {'seq'}, use_global_device_ids=true, to_apply=%add | all-reduce | flops 1152 | bytes 9216
  28.6 0.1 reshape.46
  28.7 0.1 slice.19
  28.7 0.1 eq.15
  28.8 0.1 copy.10
  28.9 0.1 lt.25
  29.0 0.1 and_reduce_fusion
  29.1 0.1 reshape.42
  29.3 0.1 reduce_or.19
  29.4 1.3 convolution_convert_fusion.1
  30.7 3.5 %copy.13 = bf16[4,8,128,512]{3,2,1,0:T(8,128)(2,1)} copy(bf16[4,8,128,512]{3,1,2,0:T(8,128)(2,1)S(1)} %bitcast.44) | data formatting | bytes 8388608
  34.2 0.0 copy-start
  34.2 8.5 %all-to-all-start = ((bf16[32,128,512]{2,1,0:T(8,128)(2,1)}), bf16[32,128,512]{2,1,0:T(8,128)(2,1)}, u32[]{:S(2)}, u32[]{:S(2)}) async-start(bf16[32,128,512]{2,1,0:T(8,128)(2,1)} %bitcast.42), calls=%async_computation | async-start | bytes 8388608 | tf_op jit(solution)/shard_map/all_to_all | solution.py:148
  42.8 0.0 copy-done
  42.8 0.4 reshape_squeeze.11
  43.1 1.3 convolution_convert_fusion
  44.5 3.5 %copy.14 = bf16[4,8,128,512]{3,2,1,0:T(8,128)(2,1)} copy(bf16[4,8,128,512]{3,1,2,0:T(8,128)(2,1)S(1)} %bitcast.43) | data formatting | bytes 8388608
  47.9 54.0 %all-to-all-done.far_k_ref = bf16[32,128,512]{2,1,0:T(8,128)(2,1)} async-done(((bf16[32,128,512]{2,1,0:T(8,128)(2,1)}), bf16[32,128,512]{2,1,0:T(8,128)(2,1)}, u32[]{:S(2)}, u32[]{:S(2)}) %all-to-all-start) | async-done | bytes 4194336 | tf_op jit(solution)/shard_map/all_to_all | solution.py:148
  101.9 0.0 copy-start.1
  101.9 5.7 %all-to-all-start.1 = ((bf16[32,128,512]{2,1,0:T(8,128)(2,1)}), bf16[32,128,512]{2,1,0:T(8,128)(2,1)}, u32[]{:S(2)}, u32[]{:S(2)}) async-start(bf16[32,128,512]{2,1,0:T(8,128)(2,1)} %bitcast.41), calls=%async_computation.1 | async-start | bytes 8388608 | tf_op jit(solution)/shard_map/all_to_all | solution.py:148
  108.3 0.0 copy-done.1
  108.3 0.6 add_select_fusion.place
  108.9 0.0 all-gather.4.cloned.1.call-done
  108.9 1.6 dynamic-slice_bitcast_fusion.reg_ref
  110.5 49.3 %all-to-all-done.1.far_v_ref = bf16[32,128,512]{2,1,0:T(8,128)(2,1)} async-done(((bf16[32,128,512]{2,1,0:T(8,128)(2,1)}), bf16[32,128,512]{2,1,0:T(8,128)(2,1)}, u32[]{:S(2)}, u32[]{:S(2)}) %all-to-all-start.1) | async-done | bytes 4194336 | tf_op jit(solution)/shard_map/all_to_all | solution.py:148
  159.8 44.4 %attention.1 = bf16[512,3584]{1,0:T(8,128)(2,1)} custom-call(s32[4,8]{1,0:T(4,128)} %add_select_fusion.place, s32[4]{0:T(128)} %bitcast.51, s32[4]{0:T(128)} %bitcast.52, bf16[512,3584]{1,0:T(8,128)(2,1)} %bitcast.45, bf16[512,512]{1,0:T(8,128)(2,1)} %bitcast.46, bf16[512,512]{1,0:T(8,128)(2,1)} %bitcast.47, ...), custom_call_target="tpu_custom_call" | custom-call | tf_op jit(solution)/shard_map/attention/pallas_call | solution.py:100
  (3 shorter events, 0.0 us)
Async XLA Ops:
  6.5 102.4 %all-gather.4.cloned.1.call-start = ((), (), s32[]{:S(2)}) async-start(), calls=%async_computation.2 | async-start | bytes 4325376 | tf_op jit(solution)/shard_map/all_gather | solution.py:22
  34.2 8.5 %copy-start = (bf16[1,512,512]{2,1,0:T(8,128)(2,1)S(1)}, bf16[1,512,512]{2,1,0:T(8,128)(2,1)}, u32[]{:S(2)}) copy-start(bf16[1,512,512]{2,1,0:T(8,128)(2,1)} %param.9) | copy-start | bytes 1572868
  34.2 67.7 %all-to-all-start = ((bf16[32,128,512]{2,1,0:T(8,128)(2,1)}), bf16[32,128,512]{2,1,0:T(8,128)(2,1)}, u32[]{:S(2)}, u32[]{:S(2)}) async-start(bf16[32,128,512]{2,1,0:T(8,128)(2,1)} %bitcast.42), calls=%async_computation | async-start | bytes 8388608 | tf_op jit(solution)/shard_map/all_to_all | solution.py:148
  101.9 6.4 %copy-start.1 = (s32[1,4,8]{2,1,0:T(4,128)S(1)}, s32[1,4,8]{2,1,0:T(4,128)}, u32[]{:S(2)}) copy-start(s32[1,4,8]{2,1,0:T(4,128)} %param.11) | copy-start | bytes 388
  101.9 57.9 %all-to-all-start.1 = ((bf16[32,128,512]{2,1,0:T(8,128)(2,1)}), bf16[32,128,512]{2,1,0:T(8,128)(2,1)}, u32[]{:S(2)}, u32[]{:S(2)}) async-start(bf16[32,128,512]{2,1,0:T(8,128)(2,1)} %bitcast.41), calls=%async_computation.1 | async-start | bytes 8388608 | tf_op jit(solution)/shard_map/all_to_all | solution.py:148
Sparse Core Ops, SparseCore 0:
  9.9 87.2 all-gather.3

commit v2 on v1

v2 whole, which is shorter than its diff:
```python
import math

import jax
import jax.numpy as jnp
from jax import lax
from jax.experimental import pallas as pl
from jax.experimental.pallas import tpu as pltpu
from jax.sharding import PartitionSpec as P

QUERY_HEADS = 28
KEY_VALUE_HEADS = 4
HEAD_SIZE = 128
REG = 64
GROUP = QUERY_HEADS // KEY_VALUE_HEADS
SCALE = math.log2(math.e) / math.sqrt(HEAD_SIZE)


very_low = -1e30


def dot_t(a, b):
    return lax.dot_general(a, b, (((1,), (1,)), ((), ())), preferred_element_type=jnp.float32)


def attend(q, reg_k, reg_v, own_k, own_v, far, is_image):
    rows = q.shape[0]
    stacked = jnp.concatenate(
        [q[:, g * HEAD_SIZE : (g + 1) * HEAD_SIZE] for g in range(GROUP)], axis=0
    )
    reg_keys = jnp.concatenate([reg_k, reg_k], axis=0)
    zero = jnp.zeros((rows, HEAD_SIZE), jnp.bfloat16)
    ones = jnp.ones((rows, HEAD_SIZE), jnp.bfloat16)
    half = jnp.concatenate([ones[:REG], zero[:REG]], axis=0)
    reg_values = jnp.concatenate([reg_v, zero[:REG]], axis=0)
    slots = [(own_k, own_v, ones), (reg_keys, reg_values, half)]
    slots += far
    visible = lax.broadcasted_iota(jnp.int32, (rows, rows), 1) <= (
        lax.broadcasted_iota(jnp.int32, (rows, rows), 0) + is_image * rows
    )
    seen = jnp.concatenate([visible] * GROUP, axis=0)
    scores = []
    for i in range(0, len(slots), 2):
        scores.append(dot_t(stacked, jnp.concatenate([slots[i][0], slots[i + 1][0]], axis=0)))
    scores[0] = jnp.concatenate(
        [jnp.where(seen, scores[0][:, :rows], very_low), scores[0][:, rows:]], axis=1
    )
    top = scores[0]
    for s in scores[1:]:
        top = jnp.maximum(top, s)
    top = jnp.max(top, axis=1, keepdims=True)
    total = None
    for i, s in enumerate(scores):
        weights = jnp.exp2((s - top) * SCALE).astype(jnp.bfloat16)
        a, b = slots[2 * i], slots[2 * i + 1]
        rhs = jnp.concatenate(
            [jnp.concatenate([a[1], a[2]], axis=1), jnp.concatenate([b[1], b[2]], axis=1)], axis=0
        )
        part = jnp.dot(weights, rhs, preferred_element_type=jnp.float32)
        total = part if total is None else total + part
    merged = (total[:, :HEAD_SIZE] / total[:, HEAD_SIZE:]).astype(jnp.bfloat16)
    return jnp.concatenate([merged[g * rows : (g + 1) * rows] for g in range(GROUP)], axis=1)


SIDE = 4
CORES = 2
SENDERS = SIDE * CORES


def layer_kernel(
    q_hbm,
    k_hbm,
    v_hbm,
    lists,
    counts,
    image,
    owner,
    out_hbm,
    q_here,
    out_here,
    gk0,
    gk1,
    gk2,
    gk3,
    gv0,
    gv1,
    gv2,
    gv3,
    rk0,
    rk1,
    rk2,
    rk3,
    rv0,
    rv1,
    rv2,
    rv3,
    outgoing,
    passing,
    asks_a,
    asks_b,
    asks_a_s,
    asks_b_s,
    marks,
    table_sem,
    load_sem,
    q_sem,
    out_sem,
    ask_send,
    ask_recv,
    ring_send,
    ring_recv,
    sel_send,
    sel_recv,
    pass_send,
    pass_recv,
):
    gathered = ((gk0, gk1, gk2, gk3), (gv0, gv1, gv2, gv3))
    received = ((rk0, rk1, rk2, rk3), (rv0, rv1, rv2, rv3))
    samp = lax.axis_index("samp")
    me = lax.axis_index("seq")
    x = me // SENDERS
    y = (me // CORES) % SIDE
    k = me % CORES
    blocks, slots = lists.shape
    rows = k_hbm.shape[0] * k_hbm.shape[1] // blocks
    width = GROUP * HEAD_SIZE

    def flag(b, t):
        return jnp.minimum(jnp.maximum(counts[b] - t, 0), 1)

    def device(c, place, core):
        if c == 0:
            return x * SENDERS + place * CORES + core
        return place * SENDERS + y * CORES + core

    def source(c, place):
        if c == 0:
            return place * SENDERS + y * CORES + k
        return x * SENDERS + place * CORES + k

    first = (x, y)
    second = (y, x)
    mine = (y * CORES + k, x * CORES + k)

    def remote(src, dst, send_sem, recv_sem, target):
        return pltpu.make_async_remote_copy(
            src_ref=src,
            dst_ref=dst,
            send_sem=send_sem,
            recv_sem=recv_sem,
            device_id=(samp, target),
            device_id_type=pl.DeviceIdType.MESH,
        )

    def load(c, h):
        hbm = (k_hbm, v_hbm)[c]
        return pltpu.make_async_copy(
            hbm.at[:, :, pl.ds(h * HEAD_SIZE, HEAD_SIZE)],
            gathered[c][h].at[first[c]],
            load_sem.at[c, h],
        )

    def load_q(h):
        cols = pl.ds(h * width, width)
        return pltpu.make_async_copy(q_hbm.at[:, cols], q_here.at[:, cols], q_sem.at[h])

    for h in range(KEY_VALUE_HEADS):
        for c in range(2):
            load(c, h).start()
    for h in range(KEY_VALUE_HEADS):
        load_q(h).start()

    lanes = lax.broadcasted_iota(jnp.int32, (1, 128), 1)
    asks = jnp.zeros((1, 128), jnp.int32)
    for b in range(blocks):
        for t in range(slots):
            entry = lists[b, t]
            used = flag(b, t)
            asks = jnp.where(lanes == (entry >> 2) * used + used - 1, entry & 3, asks)
    marks[0] = jnp.zeros((rows, HEAD_SIZE), jnp.bfloat16)
    marks[1] = jnp.ones((rows, HEAD_SIZE), jnp.bfloat16)
    asks_a[mine[0]] = asks
    asks_b[mine[1]] = asks

    barrier = pltpu.get_barrier_semaphore()
    greeted = []
    for i in range(1, SENDERS):
        greeted.append(x * SENDERS + (mine[0] + i) % SENDERS)
    for i in range(1, SIDE):
        for core in range(CORES):
            greeted.append(((x + i) % SIDE) * SENDERS + y * CORES + core)
    for target in greeted:
        pl.semaphore_signal(
            barrier, inc=1, device_id=(samp, target), device_id_type=pl.DeviceIdType.MESH
        )
    pl.semaphore_wait(barrier, len(greeted))

    tables = (asks_a, asks_b)

    def ask(c, other):
        return remote(
            tables[c].at[mine[c]],
            tables[c].at[mine[c]],
            ask_send.at[c, other],
            ask_recv.at[c, mine[c]],
            device(c, other // CORES, other % CORES),
        )

    for c in range(2):
        for i in range(1, SENDERS):
            ask(c, (mine[c] + i) % SENDERS).start()

    def ring(c, h, kind):
        step = 1 if kind % 2 == 0 else -1
        at = first[c]
        ref = gathered[c][h]
        if kind < 2:
            part = ref.at[at]
        else:
            part = ref.at[(at - step) % SIDE, pl.ds((kind - 2) * blocks, blocks)]
        return remote(
            part,
            part,
            ring_send.at[c, h, kind],
            ring_recv.at[c, h, kind],
            source(c, (at + step) % SIDE),
        )

    def ring_arrived(c, h, kind):
        step = 1 if kind % 2 == 0 else -1
        at = first[c]
        ref = gathered[c][h]
        if kind < 2:
            part = ref.at[(at - step) % SIDE]
        else:
            part = ref.at[(at - 2 * step) % SIDE, pl.ds((kind - 2) * blocks, blocks)]
        remote(
            part,
            part,
            ring_send.at[c, h, kind],
            ring_recv.at[c, h, kind],
            source(c, (at + step) % SIDE),
        ).wait_recv()

    def start_ring(h):
        for c in range(2):
            load(c, h).wait()
            ring(c, h, 0).start()
            ring(c, h, 1).start()

    def pass_ring(h):
        for kind in range(2):
            for c in range(2):
                ring_arrived(c, h, kind)
                ring(c, h, kind + 2).start()

    root = owner[0]
    reg_place = (root >> 3, (root >> 1) & 3)
    reg_sender = (root & 7, (root >> 3) * CORES + (root & 1))

    def first_leg(c, h, way):
        step = 1 if way == 0 else -1
        at = second[c]
        return remote(
            outgoing.at[c, h, ((at + 2) % SIDE) * CORES + way],
            passing.at[c, h, way],
            pass_send.at[c, h, way],
            pass_recv.at[c, h, way],
            device(c, (at + step) % SIDE, k),
        )

    def direct(c, h, role):
        at = second[c]
        if role == 4:
            place, core = at, 1 - k
        else:
            place, core = (at + (1 if role < 2 else -1)) % SIDE, role % CORES
        return remote(
            outgoing.at[c, h, place * CORES + core],
            received[c][h].at[mine[c]],
            sel_send.at[c, h, role],
            sel_recv.at[c, h, mine[c]],
            device(c, place, core),
        )

    def last_leg(c, h, way):
        step = 1 if way == 0 else -1
        at = second[c]
        origin = ((at - step) % SIDE) * CORES + k
        return remote(
            passing.at[c, h, way],
            received[c][h].at[origin],
            sel_send.at[c, h, 5 + way],
            sel_recv.at[c, h, origin],
            device(c, (at + step) % SIDE, way),
        )

    def select(h):
        for c in range(2):
            ring_arrived(c, h, 2)
            ring_arrived(c, h, 3)
        for c in range(2):
            ref = gathered[c][h]
            table = (asks_a_s, asks_b_s)[c]
            spots = [source(c, s) for s in range(SIDE)]

            @pl.loop(0, SENDERS)
            def _(d):
                for s in range(SIDE):
                    wanted = table[d, 0, spots[s]]
                    outgoing[c, h, d, 2 * s] = ref[s, 2 * wanted]
                    outgoing[c, h, d, 2 * s + 1] = ref[s, 2 * wanted + 1]
                outgoing[c, h, d, 2 * SIDE] = ref[reg_place[c], 0]

        for c in range(2):
            first_leg(c, h, 0).start()
            first_leg(c, h, 1).start()
        for role in range(5):
            for c in range(2):
                direct(c, h, role).start()
        for c in range(2):
            received[c][h][mine[c]] = outgoing[c, h, mine[c]]

    def pass_on(h):
        for way in range(2):
            for c in range(2):
                first_leg(c, h, way).wait_recv()
                last_leg(c, h, way).start()

    def all_here(h):
        load_q(h).wait()
        for c in range(2):
            for i in range(1, SENDERS):
                origin = (mine[c] + i) % SENDERS
                remote(
                    received[c][h].at[origin],
                    received[c][h].at[origin],
                    sel_send.at[c, h, 0],
                    sel_recv.at[c, h, origin],
                    device(c, origin // CORES, origin % CORES),
                ).wait_recv()
        for i in range(2):
            received[0][h][SENDERS, i] = received[0][h][reg_sender[0], 2 * SIDE]
            received[1][h][SENDERS, i] = jnp.zeros((REG, HEAD_SIZE), jnp.bfloat16)

    def store(h, b):
        return pltpu.make_async_copy(
            out_here.at[h * blocks + b],
            out_hbm.at[pl.ds(pl.multiple_of(b * rows, rows), rows), pl.ds(h * width, width)],
            out_sem.at[h * blocks + b],
        )

    def whole(ref, i, j):
        return jnp.concatenate([ref[i, 2 * j], ref[i, 2 * j + 1]], axis=0)

    def compute(h, start, stop):
        keys, values = received[0][h], received[1][h]

        @pl.loop(start, stop)
        def _(b):
            here = pl.ds(pl.multiple_of(b * rows, rows), rows)
            far = []
            for t in range(slots):
                o = lists[b, t] >> 2
                used = flag(b, t)
                spare = SENDERS * (1 - used)
                ox, oy, ok = o >> 3, (o >> 1) & 3, o & 1
                far.append(
                    (
                        whole(keys, (o & 7) * used + spare, ox * used),
                        whole(values, (ox * CORES + ok) * used + spare, oy * used),
                        marks[used],
                    )
                )
            out_here[h * blocks + b] = attend(
                q_here[here, pl.ds(h * width, width)],
                keys[reg_sender[0], 2 * SIDE],
                values[reg_sender[1], 2 * SIDE],
                whole(gathered[0][h], x, b),
                whole(gathered[1][h], y, b),
                far,
                image[b],
            )
            store(h, b).start()

    half = blocks // 2
    start_ring(0)
    start_ring(1)
    pass_ring(0)
    start_ring(2)
    pass_ring(1)
    start_ring(3)
    for c in range(2):
        for i in range(1, SENDERS):
            other = (mine[c] + i) % SENDERS
            remote(
                tables[c].at[other],
                tables[c].at[other],
                ask_send.at[c, other],
                ask_recv.at[c, other],
                device(c, other // CORES, other % CORES),
            ).wait_recv()
    to_scalars = (
        pltpu.make_async_copy(asks_a, asks_a_s, table_sem.at[0]),
        pltpu.make_async_copy(asks_b, asks_b_s, table_sem.at[1]),
    )
    for copy in to_scalars:
        copy.start()
    for copy in to_scalars:
        copy.wait()
    select(0)
    pass_ring(2)
    pass_on(0)
    pass_ring(3)
    select(1)
    for h in range(KEY_VALUE_HEADS):
        all_here(h)
        compute(h, 0, half)
        if h + 1 < KEY_VALUE_HEADS:
            pass_on(h + 1)
        if h + 2 < KEY_VALUE_HEADS:
            select(h + 2)
        compute(h, half, blocks)

    for c in range(2):
        for i in range(1, SENDERS):
            ask(c, (mine[c] + i) % SENDERS).wait_send()
    for h in range(KEY_VALUE_HEADS):
        for c in range(2):
            for kind in range(4):
                ring(c, h, kind).wait_send()
            for way in range(2):
                first_leg(c, h, way).wait_send()
                last_leg(c, h, way).wait_send()
            for role in range(5):
                direct(c, h, role).wait_send()
        for b in range(blocks):
            store(h, b).wait()


def layer(q, k, v, lists, counts, image, owner):
    blocks = lists.shape[0]
    rows = q.shape[0] // blocks
    width = GROUP * HEAD_SIZE
    message = (2 * SIDE + 1, REG, HEAD_SIZE)
    k = k.reshape(-1, REG, k.shape[1])
    v = v.reshape(-1, REG, v.shape[1])
    heads = KEY_VALUE_HEADS
    bf16 = jnp.bfloat16
    dma = pltpu.SemaphoreType.DMA
    return pl.pallas_call(
        layer_kernel,
        out_shape=jax.ShapeDtypeStruct(q.shape, bf16),
        in_specs=[pl.BlockSpec(memory_space=pl.ANY)] * 3
        + [pl.BlockSpec(memory_space=pltpu.SMEM)] * 4,
        out_specs=pl.BlockSpec(memory_space=pl.ANY),
        scratch_shapes=[
            pltpu.VMEM(q.shape, bf16),
            pltpu.VMEM((heads * blocks, rows, width), bf16),
        ]
        + [pltpu.VMEM((SIDE, 2 * blocks, REG, HEAD_SIZE), bf16)] * 8
        + [pltpu.VMEM((SENDERS + 1, *message), bf16)] * 8
        + [
            pltpu.VMEM((2, heads, SENDERS, *message), bf16),
            pltpu.VMEM((2, heads, 2, *message), bf16),
            pltpu.VMEM((SENDERS, 1, 128), jnp.int32),
            pltpu.VMEM((SENDERS, 1, 128), jnp.int32),
            pltpu.SMEM((SENDERS, 1, 128), jnp.int32),
            pltpu.SMEM((SENDERS, 1, 128), jnp.int32),
            pltpu.VMEM((2, rows, HEAD_SIZE), bf16),
            dma((2,)),
            dma((2, heads)),
            dma((heads,)),
            dma((heads * blocks,)),
            dma((2, SENDERS)),
            dma((2, SENDERS)),
            dma((2, heads, 4)),
            dma((2, heads, 4)),
            dma((2, heads, 7)),
            dma((2, heads, SENDERS)),
            dma((2, heads, 2)),
            dma((2, heads, 2)),
        ],
        compiler_params=pltpu.CompilerParams(
            collective_id=0, has_side_effects=True, vmem_limit_bytes=60 << 20
        ),
        name="layer",
    )(q, k, v, lists, counts, image, owner)


def per_device(queries, keys, values, reg_owner, block_lists, list_counts, image_blocks):
    out = layer(
        queries[0],
        keys[0],
        values[0],
        block_lists[0],
        list_counts[0],
        image_blocks[0],
        reg_owner,
    )
    return out[None]


def solution(mesh):
    placed = (
        P("samp", "seq", None),
        P("samp", "seq", None),
        P("samp", "seq", None),
        P("samp"),
        P("samp", "seq", None),
        P("samp", "seq"),
        P("samp", "seq"),
    )
    return jax.shard_map(
        per_device, mesh=mesh, in_specs=placed, out_specs=P("samp", "seq", None), check_vma=False
    )
```

time: 212 us -> 93.9 us (0.44)
  waiting for transfers between devices: 103 us -> 0 us
  Pallas kernels: 44.4 us -> 88.6 us
  blocking collectives: 14.7 us -> 0 us
  starting transfers between devices: 14.3 us -> 0 us
  between operations: 14.7 us -> 0.66 us
  local copies, waits for them, and re-layouts: 14.6 us -> 4.11 us
  matrix products: 2.64 us -> 0 us
  other arithmetic: 2.36 us -> 0 us
    all_to_all x2 -> x0, waiting for transfers between devices: 103 us -> none  [per_device(): lax.all_to_all(sent.reshape(devices, rows_block, kv_width), 'seq', split_...]
    pallas_call x1, Pallas kernels: 44.4 us -> 88.6 us  [layer(): pl.pallas_call(layer_kernel, out_shape=jax.ShapeDtypeStruct(q.shape, bf16...]
    unnamed x1 -> x0, blocking collectives: 14.7 us -> none
    all_to_all x2 -> x0, starting transfers between devices: 14.3 us -> none  [per_device(): lax.all_to_all(sent.reshape(devices, rows_block, kv_width), 'seq', split_...]
    unnamed x8 -> x1, local copies, waits for them, and re-layouts: 8.24 us -> 4.11 us
    dot_general x2 -> x0, matrix products: 2.64 us -> none  [per_device(): jnp.dot(selector, array.reshape(blocks_here, rows_block * kv_width), pref...]
    another operation x3 -> x0, local copies, waits for them, and re-layouts: 2.58 us -> none  [the longest x2 1.82 us: per_device(): array.reshape(blocks_here, rows_block * kv_width)]
  transfers between devices with their start and end apart: 3 -> 0, of which waited for: 2 -> 0; matrix products, arithmetic and copies ran while one was open for 8% -> 0% of each run, Pallas kernels for 0% -> 0%
where the time goes in v2:
time: 93.9 us; the launch traced here: 93.4 us
  Pallas kernels  88.6 us (94%)
  local copies, waits for them, and re-layouts  4.11 us (4%)
    pallas_call x1, Pallas kernels, layer(): pl.pallas_call(layer_kernel, out_shape=jax.ShapeDtypeStruct(q.shape, bf16...  88.6 us
    unnamed x1, local copies, waits for them, and re-layouts  4.11 us

profile of v2, /device:TPU:1, one launch (start us, length us, event | category | flops | bytes accessed | tf_op | source)
XLA Modules:
  0.0 93.4 jit_solution(2920737381631428758)
XLA Ops:
  0.7 88.6 %layer.1 = bf16[512,3584]{1,0:T(8,128)(2,1)} custom-call(bf16[512,3584]{1,0:T(8,128)(2,1)} %bitcast.8, bf16[8,64,512]{2,1,0:T(8,128)(2,1)} %bitcast.9, bf16[8,64,512]{2,1,0:T(8,128)(2,1)} %bitcast.10, s32[4,8]{1,0:T(4,128)} %bitcast.11, s32[4]{0:T(128)} %bitcast.12, s32[4]{0:T(128)} %bitcast.13, s32[1]{0:T(128)S(6)} %copy.9.owner), custom_call_target="tpu_custom_call" | custom-call | tf_op jit(solution)/shard_map/layer/pallas_call | solution.py:450
  89.3 4.1 %copy.10 = bf16[1,512,3584]{2,1,0:T(8,128)(2,1)} copy(bf16[1,512,3584]{2,1,0:T(8,128)(2,1)} %bitcast.7) | data formatting | bytes 7340032

commit v3 on v1

v3 whole, which is shorter than its diff:
```python
import math

import jax
import jax.numpy as jnp
from jax import lax
from jax.experimental import pallas as pl
from jax.experimental.pallas import tpu as pltpu
from jax.sharding import PartitionSpec as P

QUERY_HEADS = 28
KEY_VALUE_HEADS = 4
HEAD_SIZE = 128
REG = 64
GROUP = QUERY_HEADS // KEY_VALUE_HEADS
SCALE = math.log2(math.e) / math.sqrt(HEAD_SIZE)


very_low = -1e30


def dot_t(a, b):
    return lax.dot_general(a, b, (((1,), (1,)), ((), ())), preferred_element_type=jnp.float32)


PARTS = 4


def stacked_heads(q):
    return jnp.concatenate(
        [q[:, g * HEAD_SIZE : (g + 1) * HEAD_SIZE] for g in range(GROUP)], axis=0
    )


def spread_heads(merged, rows):
    return jnp.concatenate([merged[g * rows : (g + 1) * rows] for g in range(GROUP)], axis=1)


def paired(blocks):
    return [
        jnp.concatenate([blocks[i], blocks[i + 1]], axis=0) for i in range(0, len(blocks), 2)
    ]


def key_pairs(own_k, reg_k, far):
    return paired([own_k, jnp.concatenate([reg_k, reg_k], axis=0)] + far)


def value_pairs(own_v, reg_v, far, used):
    rows = own_v.shape[0]
    zero = jnp.zeros((rows, HEAD_SIZE), jnp.bfloat16)
    ones = jnp.ones((rows, HEAD_SIZE), jnp.bfloat16)
    half = jnp.concatenate([ones[:REG], zero[:REG]], axis=0)
    values = [own_v, jnp.concatenate([reg_v, zero[:REG]], axis=0)] + far
    marks = [ones, half] + used
    return paired([jnp.concatenate([v, m], axis=1) for v, m in zip(values, marks)])


def seen_rows(rows, is_image):
    visible = lax.broadcasted_iota(jnp.int32, (rows, rows), 1) <= (
        lax.broadcasted_iota(jnp.int32, (rows, rows), 0) + is_image * rows
    )
    return jnp.concatenate([visible] * GROUP, axis=0)


def score(stacked, keys, seen, lo, hi):
    rows = seen.shape[1]
    scores = [dot_t(stacked[lo:hi], key) for key in keys]
    own = jnp.where(seen[lo:hi], scores[0][:, :rows], very_low)
    scores[0] = jnp.concatenate([own, scores[0][:, rows:]], axis=1)
    return scores


def soften(scores):
    top = scores[0]
    for s in scores[1:]:
        top = jnp.maximum(top, s)
    top = jnp.max(top, axis=1, keepdims=True)
    return [jnp.exp2((s - top) * SCALE).astype(jnp.bfloat16) for s in scores]


def finish(weights, values):
    total = None
    for w, value in zip(weights, values):
        part = jnp.dot(w, value, preferred_element_type=jnp.float32)
        total = part if total is None else total + part
    return (total[:, :HEAD_SIZE] / total[:, HEAD_SIZE:]).astype(jnp.bfloat16)


SIDE = 4
CORES = 2
CHIP_SLOTS = SIDE * SIDE
DEVICE_X = SIDE * CORES
UNITS = 2 * KEY_VALUE_HEADS

WAYS = ((1, 0), (-1, 0), (0, 1), (0, -1))
FULL = (
    ((0, 0), None, None),
    ((1, 0), 0, 0),
    ((0, 1), 0, 2),
    ((2, 0), 1, 0),
    ((0, 2), 2, 2),
    ((2, 3), 3, 3),
)
LEAF = (
    ((0, 3), 0, 3),
    ((3, 0), 0, 1),
    ((1, 1), 1, 2),
    ((3, 1), 2, 1),
    ((2, 1), 3, 2),
    ((3, 2), 4, 1),
    ((1, 2), 4, 0),
    ((2, 2), 5, 3),
    ((3, 3), 5, 0),
    ((1, 3), 5, 1),
)
LEAVES = len(LEAF)
PLACES = len(FULL)
ASKERS = 2 * len(WAYS) + 2
PARTNER, SELF = ASKERS - 2, ASKERS - 1
REG_STEPS = 6


def layer_kernel(q_hbm, k_hbm, v_hbm, lists, counts, image, owner, out_hbm, *scratch):
    full_refs = [scratch[u * PLACES : (u + 1) * PLACES] for u in range(UNITS)]
    scratch = scratch[UNITS * PLACES :]
    received = scratch[:UNITS]
    regs_pair = scratch[UNITS : UNITS + REG_STEPS - 1]
    scratch = scratch[REG_STEPS - 1 :]
    (
        outgoing,
        asks,
        asks_s,
        marks,
        regs_in,
        regs,
        q_here,
        out_here,
        weights_here,
        table_sem,
        load_sem,
        regs_sem,
        q_sem,
        out_sem,
        ask_send,
        ask_recv,
        reg_send,
        reg_recv,
        full_send,
        full_recv,
        leaf_send,
        leaf_recv,
        pair_send,
        pair_recv,
    ) = scratch[UNITS:]
    samp = lax.axis_index("samp")
    me = lax.axis_index("seq")
    x = me // DEVICE_X
    y = (me // CORES) % SIDE
    k = me % CORES
    sign = 1 - 2 * k
    blocks, slots = lists.shape
    rows = q_hbm.shape[0] // blocks
    width = GROUP * HEAD_SIZE

    def device(px, py, core):
        return px * DEVICE_X + py * CORES + core

    partner = device(x, y, 1 - k)

    def beside(way, turn, core):
        dx, dy = WAYS[way]
        return device((x + turn * dx + SIDE) % SIDE, (y + turn * dy + SIDE) % SIDE, core)

    def slot(core, offset):
        return core * CHIP_SLOTS + offset[0] * SIDE + offset[1]

    def flag(b, t):
        return jnp.minimum(jnp.maximum(counts[b] - t, 0), 1)

    def remote(src, dst, send_sem, recv_sem, target):
        return pltpu.make_async_remote_copy(
            src_ref=src,
            dst_ref=dst,
            send_sem=send_sem,
            recv_sem=recv_sem,
            device_id=(samp, target),
            device_id_type=pl.DeviceIdType.MESH,
        )

    def load(u):
        hbm = (k_hbm, v_hbm)[u % 2]
        cols = pl.ds((u // 2) * HEAD_SIZE, HEAD_SIZE)
        return pltpu.make_async_copy(hbm.at[:, :, cols], full_refs[u][0], load_sem.at[u])

    def load_regs(c):
        hbm = (k_hbm, v_hbm)[c]
        return pltpu.make_async_copy(
            hbm.at[0, pl.ds(0, REG)], regs_in.at[c], regs_sem.at[c]
        )

    def load_q(h):
        cols = pl.ds(h * width, width)
        return pltpu.make_async_copy(q_hbm.at[:, cols], q_here.at[:, cols], q_sem.at[h])

    def full(u, f):
        _, before, way = FULL[f]
        return remote(
            full_refs[u][before],
            full_refs[u][f],
            full_send.at[u, f],
            full_recv.at[u, f],
            beside(way, sign, k),
        )

    def leaf(u, i, core):
        offset, _, way = LEAF[i]
        return remote(
            outgoing.at[u, 2 * i + core],
            received[u].at[slot(k, offset)],
            leaf_send.at[u, 2 * i + core],
            leaf_recv.at[u, k * LEAVES + i],
            beside(way, sign, core),
        )

    def across(u, f):
        return remote(
            outgoing.at[u, 2 * LEAVES + f],
            received[u].at[slot(k, FULL[f][0])],
            pair_send.at[u, f],
            pair_recv.at[u, f],
            partner,
        )

    def ask(i):
        if i == PARTNER:
            target, there = partner, PARTNER
        else:
            way, core = i // 2, i % 2
            target, there = beside(way, 1, core), 2 * (way ^ 1) + k
        return remote(
            asks.at[SELF], asks.at[there], ask_send.at[i], ask_recv.at[there], target
        )

    load(0).start()
    load(1).start()
    for c in range(2):
        load_regs(c).start()
    for u in range(2, UNITS):
        load(u).start()
    for h in range(KEY_VALUE_HEADS):
        load_q(h).start()

    marks[0] = jnp.zeros((rows, HEAD_SIZE), jnp.bfloat16)
    marks[1] = jnp.ones((rows, HEAD_SIZE), jnp.bfloat16)
    lanes = lax.broadcasted_iota(jnp.int32, (1, 128), 1)
    wanted = jnp.zeros((1, 128), jnp.int32)
    for b in range(blocks):
        for t in range(slots):
            entry = lists[b, t]
            used = flag(b, t)
            wanted = jnp.where(lanes == (entry >> 2) * used + used - 1, entry & 3, wanted)
    asks[SELF] = wanted

    barrier = pltpu.get_barrier_semaphore()
    greeted = [partner] + [beside(way, 1, core) for way in range(4) for core in range(CORES)]
    for target in greeted:
        pl.semaphore_signal(
            barrier, inc=1, device_id=(samp, target), device_id_type=pl.DeviceIdType.MESH
        )
    pl.semaphore_wait(barrier, len(greeted))

    for i in range(PARTNER + 1):
        ask(i).start()

    root = owner[0]
    sides = (
        (root ^ k) & 1,
        ((root >> 3) ^ x) & 1,
        ((root >> 4) ^ (x // 2)) & 1,
        ((root >> 1) ^ y) & 1,
        ((root >> 2) ^ (y // 2)) & 1,
    )
    reg_targets = (
        partner,
        device(x + 1 - 2 * (x % 2), y, k),
        device(SIDE - 1 - x, y, k),
        device(x, y + 1 - 2 * (y % 2), k),
        device(x, SIDE - 1 - y, k),
        partner,
    )

    def reg_copy(i):
        if i == 0:
            src, dst = regs_in.at[1 - k], regs_pair[0].at[1]
        elif i < 5:
            src, dst = regs_pair[i].at[0], regs_pair[i].at[1]
        else:
            src, dst = regs.at[k], regs.at[k]
        return remote(src, dst, reg_send.at[i], reg_recv.at[i], reg_targets[i])

    def reg_step(i):
        if i == 0:
            for c in range(2):
                load_regs(c).wait()
            regs_pair[0][0] = regs_in[k]
        else:
            reg_copy(i - 1).wait_recv()
            chosen = pair_of(i - 1)
            if i < 5:
                regs_pair[i][0] = chosen
            else:
                regs[k] = chosen
        reg_copy(i).start()

    def pair_of(i):
        return regs_pair[i][sides[i]]

    def regs_here():
        remote(
            regs.at[1 - k], regs.at[1 - k], reg_send.at[5], reg_recv.at[5], partner
        ).wait_recv()

    def give(u, f):
        ref = full_refs[u][f]
        offset = FULL[f][0]
        spot = device(
            (x - sign * offset[0] + SIDE) % SIDE, (y - sign * offset[1] + SIDE) % SIDE, k
        )
        for i, (_, before, way) in enumerate(LEAF):
            if before == f:
                turned = way + k if way % 2 == 0 else way - k
                for core in range(CORES):
                    outgoing[u, 2 * i + core] = ref[asks_s[2 * turned + core, 0, spot]]
        outgoing[u, 2 * LEAVES + f] = ref[asks_s[PARTNER, 0, spot]]
        if f:
            received[u][slot(k, offset)] = ref[asks_s[SELF, 0, spot]]
        for i, (_, before, _) in enumerate(LEAF):
            if before == f:
                for core in range(CORES):
                    leaf(u, i, core).start()
        across(u, f).start()

    def begin(u):
        load(u).wait()
        full(u, 1).start()
        full(u, 2).start()

    def stage(u, n):
        if not 0 <= u < UNITS:
            return
        if n == 0:
            give(u, 0)
        elif n == 1:
            for f in (1, 2):
                full(u, f).wait_recv()
                full(u, f + 2).start()
            give(u, 1)
            give(u, 2)
        elif n == 2:
            full(u, 3).wait_recv()
            full(u, 5).start()
            full(u, 4).wait_recv()
            give(u, 3)
            give(u, 4)
        else:
            full(u, 5).wait_recv()
            give(u, 5)

    def all_here(u):
        h = u // 2
        for core in range(CORES):
            for i in range(LEAVES):
                ref = received[u].at[slot(core, LEAF[i][0])]
                remote(
                    ref, ref, leaf_send.at[u, 0], leaf_recv.at[u, core * LEAVES + i], partner
                ).wait_recv()
        for f in range(PLACES):
            ref = received[u].at[slot(1 - k, FULL[f][0])]
            remote(ref, ref, pair_send.at[u, f], pair_recv.at[u, f], partner).wait_recv()
        if u % 2 == 0:
            load_q(h).wait()
            spare = regs[0, :, pl.ds(h * HEAD_SIZE, HEAD_SIZE)]
            received[u][slot(k, (0, 0))] = jnp.concatenate([spare, spare], axis=0)
        else:
            received[u][slot(k, (0, 0))] = jnp.zeros((rows, HEAD_SIZE), jnp.bfloat16)

    def store(h, b):
        return pltpu.make_async_copy(
            out_here.at[h * blocks + b],
            out_hbm.at[pl.ds(pl.multiple_of(b * rows, rows), rows), pl.ds(h * width, width)],
            out_sem.at[h * blocks + b],
        )

    def far_slots(b):
        places = []
        for t in range(slots):
            o = lists[b, t] >> 2
            used = flag(b, t)
            core = o & 1
            turn = 1 - 2 * core
            dx = ((x - (o >> 3)) * turn) & 3
            dy = ((y - (o >> 1)) * turn) & 3
            place = core * CHIP_SLOTS + dx * SIDE + dy
            places.append((place * used + slot(k, (0, 0)) * (1 - used), used))
        return places

    def keys_of(h, b, places):
        return key_pairs(
            full_refs[2 * h][0][b],
            regs[0, :, pl.ds(h * HEAD_SIZE, HEAD_SIZE)],
            [received[2 * h][place] for place, _ in places],
        )

    def values_of(h, b, places):
        return value_pairs(
            full_refs[2 * h + 1][0][b],
            regs[1, :, pl.ds(h * HEAD_SIZE, HEAD_SIZE)],
            [received[2 * h + 1][place] for place, _ in places],
            [marks[used] for _, used in places],
        )

    def queries_of(h, b):
        here = pl.ds(pl.multiple_of(b * rows, rows), rows)
        return stacked_heads(q_here[here, pl.ds(h * width, width)])

    part = rows * GROUP // PARTS

    def compute(h, start, stop):
        @pl.loop(start, stop)
        def _(b):
            places = far_slots(b)
            stacked = queries_of(h, b)
            keys, values = keys_of(h, b, places), values_of(h, b, places)
            seen = seen_rows(rows, image[b])
            scores = [score(stacked, keys, seen, 0, part)]
            outs = []
            for n in range(PARTS):
                if n + 1 < PARTS:
                    scores.append(
                        score(stacked, keys, seen, (n + 1) * part, (n + 2) * part)
                    )
                outs.append(finish(soften(scores[n]), values))
            out_here[h * blocks + b] = spread_heads(jnp.concatenate(outs, axis=0), rows)
            store(h, b).start()

    def compute_weights(h):
        @pl.loop(0, blocks)
        def _(b):
            stacked = queries_of(h, b)
            keys = keys_of(h, b, far_slots(b))
            seen = seen_rows(rows, image[b])
            scores = [score(stacked, keys, seen, 0, part)]
            for n in range(PARTS):
                if n + 1 < PARTS:
                    scores.append(
                        score(stacked, keys, seen, (n + 1) * part, (n + 2) * part)
                    )
                for i, w in enumerate(soften(scores[n])):
                    weights_here[b, i, pl.ds(n * part, part)] = w

    def compute_outputs(h):
        @pl.loop(0, blocks)
        def _(b):
            values = values_of(h, b, far_slots(b))
            pairs = len(values)
            outs = finish([weights_here[b, i] for i in range(pairs)], values)
            out_here[h * blocks + b] = spread_heads(outs, rows)
            store(h, b).start()

    begin(0)
    begin(1)
    reg_step(0)
    begin(2)
    for i in range(PARTNER + 1):
        ref = asks.at[i]
        remote(ref, ref, ask_send.at[i], ask_recv.at[i], partner).wait_recv()
    to_scalars = pltpu.make_async_copy(asks, asks_s, table_sem.at[0])
    to_scalars.start()
    to_scalars.wait()
    stage(0, 0)
    stage(1, 0)
    reg_step(1)
    stage(2, 0)
    last = KEY_VALUE_HEADS - 1
    half = blocks // 2
    for t in range(UNITS + 2):
        stage(t, 1)
        stage(t - 1, 2)
        stage(t - 2, 3)
        if t + 3 < UNITS:
            begin(t + 3)
            stage(t + 3, 0)
        if t + 2 < REG_STEPS:
            reg_step(t + 2)
        if t == REG_STEPS - 2:
            regs_here()
        if t >= 4:
            h = t // 2 - 2
            if t % 2 == 0:
                all_here(2 * h)
                all_here(2 * h + 1)
                compute(h, 0, half)
            else:
                compute(h, half, blocks)
    all_here(2 * last)
    compute_weights(last)
    all_here(2 * last + 1)
    compute_outputs(last)

    for i in range(PARTNER + 1):
        ask(i).wait_send()
    for i in range(REG_STEPS):
        reg_copy(i).wait_send()
    for u in range(UNITS):
        for f in range(1, PLACES):
            full(u, f).wait_send()
        for f in range(PLACES):
            across(u, f).wait_send()
        for i in range(LEAVES):
            for core in range(CORES):
                leaf(u, i, core).wait_send()
    for h in range(KEY_VALUE_HEADS):
        for b in range(blocks):
            store(h, b).wait()


def layer(q, k, v, lists, counts, image, owner):
    blocks, slots = lists.shape
    rows = q.shape[0] // blocks
    kv_width = k.shape[1]
    width = GROUP * HEAD_SIZE
    heads = KEY_VALUE_HEADS
    bf16 = jnp.bfloat16
    dma = pltpu.SemaphoreType.DMA
    return pl.pallas_call(
        layer_kernel,
        out_shape=jax.ShapeDtypeStruct(q.shape, bf16),
        in_specs=[pl.BlockSpec(memory_space=pl.ANY)] * 3
        + [pl.BlockSpec(memory_space=pltpu.SMEM)] * 4,
        out_specs=pl.BlockSpec(memory_space=pl.ANY),
        scratch_shapes=[pltpu.VMEM((blocks, rows, HEAD_SIZE), bf16)] * (UNITS * PLACES)
        + [pltpu.VMEM((CORES * CHIP_SLOTS, rows, HEAD_SIZE), bf16)] * UNITS
        + [pltpu.VMEM((2, REG, kv_width), bf16)] * (REG_STEPS - 1)
        + [
            pltpu.VMEM((UNITS, 2 * LEAVES + PLACES, rows, HEAD_SIZE), bf16),
            pltpu.VMEM((ASKERS, 1, 128), jnp.int32),
            pltpu.SMEM((ASKERS, 1, 128), jnp.int32),
            pltpu.VMEM((2, rows, HEAD_SIZE), bf16),
            pltpu.VMEM((2, REG, kv_width), bf16),
            pltpu.VMEM((2, REG, kv_width), bf16),
            pltpu.VMEM(q.shape, bf16),
            pltpu.VMEM((heads * blocks, rows, width), bf16),
            pltpu.VMEM((blocks, (slots + 2) // 2, GROUP * rows, 2 * rows), bf16),
            dma((1,)),
            dma((UNITS,)),
            dma((2,)),
            dma((heads,)),
            dma((heads * blocks,)),
            dma((PARTNER + 1,)),
            dma((PARTNER + 1,)),
            dma((REG_STEPS,)),
            dma((REG_STEPS,)),
            dma((UNITS, PLACES)),
            dma((UNITS, PLACES)),
            dma((UNITS, 2 * LEAVES)),
            dma((UNITS, 2 * LEAVES)),
            dma((UNITS, PLACES)),
            dma((UNITS, PLACES)),
        ],
        compiler_params=pltpu.CompilerParams(
            collective_id=0, has_side_effects=True, vmem_limit_bytes=62 << 20
        ),
        name="layer",
    )(
        q,
        k.reshape(blocks, rows, kv_width),
        v.reshape(blocks, rows, kv_width),
        lists,
        counts,
        image,
        owner,
    )


def per_device(queries, keys, values, reg_owner, block_lists, list_counts, image_blocks):
    out = layer(
        queries[0],
        keys[0],
        values[0],
        block_lists[0],
        list_counts[0],
        image_blocks[0],
        reg_owner,
    )
    return out[None]


def solution(mesh):
    placed = (
        P("samp", "seq", None),
        P("samp", "seq", None),
        P("samp", "seq", None),
        P("samp"),
        P("samp", "seq", None),
        P("samp", "seq"),
        P("samp", "seq"),
    )
    return jax.shard_map(
        per_device, mesh=mesh, in_specs=placed, out_specs=P("samp", "seq", None), check_vma=False
    )
```

time: 212 us -> 90.9 us (0.43)
  waiting for transfers between devices: 103 us -> 0 us
  Pallas kernels: 44.4 us -> 86 us
  blocking collectives: 14.7 us -> 0 us
  starting transfers between devices: 14.3 us -> 0 us
  between operations: 14.7 us -> 0.66 us
  local copies, waits for them, and re-layouts: 14.6 us -> 4.11 us
  matrix products: 2.64 us -> 0 us
  other arithmetic: 2.36 us -> 0 us
    all_to_all x2 -> x0, waiting for transfers between devices: 103 us -> none  [per_device(): lax.all_to_all(sent.reshape(devices, rows_block, kv_width), 'seq', split_...]
    pallas_call x1, Pallas kernels: 44.4 us -> 86 us  [layer(): pl.pallas_call(layer_kernel, out_shape=jax.ShapeDtypeStruct(q.shape, bf16...]
    unnamed x1 -> x0, blocking collectives: 14.7 us -> none
    all_to_all x2 -> x0, starting transfers between devices: 14.3 us -> none  [per_device(): lax.all_to_all(sent.reshape(devices, rows_block, kv_width), 'seq', split_...]
    unnamed x8 -> x1, local copies, waits for them, and re-layouts: 8.24 us -> 4.11 us
    dot_general x2 -> x0, matrix products: 2.64 us -> none  [per_device(): jnp.dot(selector, array.reshape(blocks_here, rows_block * kv_width), pref...]
    another operation x3 -> x0, local copies, waits for them, and re-layouts: 2.58 us -> none  [the longest x2 1.82 us: per_device(): array.reshape(blocks_here, rows_block * kv_width)]
  transfers between devices with their start and end apart: 3 -> 0, of which waited for: 2 -> 0; matrix products, arithmetic and copies ran while one was open for 8% -> 0% of each run, Pallas kernels for 0% -> 0%
where the time goes in v3:
time: 90.9 us; the launch traced here: 90.8 us
  Pallas kernels  86 us (95%)
  local copies, waits for them, and re-layouts  4.11 us (5%)
    pallas_call x1, Pallas kernels, layer(): pl.pallas_call(layer_kernel, out_shape=jax.ShapeDtypeStruct(q.shape, bf16...  86 us
    unnamed x1, local copies, waits for them, and re-layouts  4.11 us

profile of v3, /device:TPU:1, one launch (start us, length us, event | category | flops | bytes accessed | tf_op | source)
XLA Modules:
  0.0 90.8 jit_solution(6526285699834500987)
XLA Ops:
  0.7 86.0 %layer.1 = bf16[512,3584]{1,0:T(8,128)(2,1)} custom-call(bf16[512,3584]{1,0:T(8,128)(2,1)} %bitcast.8, bf16[4,128,512]{2,1,0:T(8,128)(2,1)} %bitcast.9, bf16[4,128,512]{2,1,0:T(8,128)(2,1)} %bitcast.10, s32[4,8]{1,0:T(4,128)} %bitcast.11, s32[4]{0:T(128)} %bitcast.12, s32[4]{0:T(128)} %bitcast.13, s32[1]{0:T(128)S(6)} %copy.9.owner), custom_call_target="tpu_custom_call" | custom-call | tf_op jit(solution)/shard_map/layer/pallas_call | solution.py:535
  86.6 4.1 %copy.10 = bf16[1,512,3584]{2,1,0:T(8,128)(2,1)} copy(bf16[1,512,3584]{2,1,0:T(8,128)(2,1)} %bitcast.7) | data formatting | bytes 7340032

commit v4 on v3

--- a/solution.py
+++ b/solution.py
@@ -90,7 +90,11 @@
 CORES = 2
 CHIP_SLOTS = SIDE * SIDE
 DEVICE_X = SIDE * CORES
-UNITS = 2 * KEY_VALUE_HEADS
+ORDER = ((0, 0), (0, 1), (1, 0), (1, 1), (2, 0), (3, 0), (2, 1), (3, 1))
+UNITS = len(ORDER)
+KEYS = {h: u for u, (h, c) in enumerate(ORDER) if c == 0}
+VALUES = {h: u for u, (h, c) in enumerate(ORDER) if c == 1}
+LEAD = 2
 
 WAYS = ((1, 0), (-1, 0), (0, 1), (0, -1))
 FULL = (
@@ -115,12 +119,18 @@
 )
 LEAVES = len(LEAF)
 PLACES = len(FULL)
+MESSAGES = 2 * LEAVES + PLACES
 ASKERS = 2 * len(WAYS) + 2
 PARTNER, SELF = ASKERS - 2, ASKERS - 1
-REG_STEPS = 6
-
-
-def layer_kernel(q_hbm, k_hbm, v_hbm, lists, counts, image, owner, out_hbm, *scratch):
+REG_STEPS = 5
+REG_COPIES = REG_STEPS + 2
+
+
+def layer_kernel(
+    q_hbm, k_hbm, v_hbm, lists_hbm, counts_hbm, image_hbm, owner_hbm, out_hbm, *scratch
+):
+    lists, counts, image, owner, small_sem = scratch[:5]
+    scratch = scratch[5:]
     full_refs = [scratch[u * PLACES : (u + 1) * PLACES] for u in range(UNITS)]
     scratch = scratch[UNITS * PLACES :]
     received = scratch[:UNITS]
@@ -147,10 +157,8 @@
         reg_recv,
         full_send,
         full_recv,
-        leaf_send,
-        leaf_recv,
-        pair_send,
-        pair_recv,
+        unit_send,
+        unit_recv,
     ) = scratch[UNITS:]
     samp = lax.axis_index("samp")
     me = lax.axis_index("seq")
@@ -188,8 +196,9 @@
         )
 
     def load(u):
-        hbm = (k_hbm, v_hbm)[u % 2]
-        cols = pl.ds((u // 2) * HEAD_SIZE, HEAD_SIZE)
+        h, c = ORDER[u]
+        hbm = (k_hbm, v_hbm)[c]
+        cols = pl.ds(h * HEAD_SIZE, HEAD_SIZE)
         return pltpu.make_async_copy(hbm.at[:, :, cols], full_refs[u][0], load_sem.at[u])
 
     def load_regs(c):
@@ -207,7 +216,7 @@
         return remote(
             full_refs[u][before],
             full_refs[u][f],
-            full_send.at[u, f],
+            full_send.at[u],
             full_recv.at[u, f],
             beside(way, sign, k),
         )
@@ -217,8 +226,8 @@
         return remote(
             outgoing.at[u, 2 * i + core],
             received[u].at[slot(k, offset)],
-            leaf_send.at[u, 2 * i + core],
-            leaf_recv.at[u, k * LEAVES + i],
+            unit_send.at[u],
+            unit_recv.at[u],
             beside(way, sign, core),
         )
 
@@ -226,8 +235,8 @@
         return remote(
             outgoing.at[u, 2 * LEAVES + f],
             received[u].at[slot(k, FULL[f][0])],
-            pair_send.at[u, f],
-            pair_recv.at[u, f],
+            unit_send.at[u],
+            unit_recv.at[u],
             partner,
         )
 
@@ -238,13 +247,32 @@
             way, core = i // 2, i % 2
             target, there = beside(way, 1, core), 2 * (way ^ 1) + k
         return remote(
-            asks.at[SELF], asks.at[there], ask_send.at[i], ask_recv.at[there], target
-        )
-
+            asks.at[SELF], asks.at[there], ask_send.at[0], ask_recv.at[0], target
+        )
+
+    barrier = pltpu.get_barrier_semaphore()
+    greeted = [partner] + [beside(way, 1, core) for way in range(4) for core in range(CORES)]
+    for target in greeted:
+        pl.semaphore_signal(
+            barrier, inc=1, device_id=(samp, target), device_id_type=pl.DeviceIdType.MESH
+        )
+    small = [
+        pltpu.make_async_copy(src, dst, small_sem.at[i])
+        for i, (src, dst) in enumerate(
+            (
+                (lists_hbm, lists),
+                (counts_hbm, counts),
+                (image_hbm, image),
+                (owner_hbm, owner),
+            )
+        )
+    ]
+    for copy in small:
+        copy.start()
+    for c in range(2):
+        load_regs(c).start()
     load(0).start()
     load(1).start()
-    for c in range(2):
-        load_regs(c).start()
     for u in range(2, UNITS):
         load(u).start()
     for h in range(KEY_VALUE_HEADS):
@@ -252,6 +280,8 @@
 
     marks[0] = jnp.zeros((rows, HEAD_SIZE), jnp.bfloat16)
     marks[1] = jnp.ones((rows, HEAD_SIZE), jnp.bfloat16)
+    for copy in small:
+        copy.wait()
     lanes = lax.broadcasted_iota(jnp.int32, (1, 128), 1)
     wanted = jnp.zeros((1, 128), jnp.int32)
     for b in range(blocks):
@@ -261,12 +291,6 @@
             wanted = jnp.where(lanes == (entry >> 2) * used + used - 1, entry & 3, wanted)
     asks[SELF] = wanted
 
-    barrier = pltpu.get_barrier_semaphore()
-    greeted = [partner] + [beside(way, 1, core) for way in range(4) for core in range(CORES)]
-    for target in greeted:
-        pl.semaphore_signal(
-            barrier, inc=1, device_id=(samp, target), device_id_type=pl.DeviceIdType.MESH
-        )
     pl.semaphore_wait(barrier, len(greeted))
 
     for i in range(PARTNER + 1):
@@ -274,15 +298,16 @@
 
     root = owner[0]
     sides = (
-        (root ^ k) & 1,
-        ((root >> 3) ^ x) & 1,
+        (((root >> 3) ^ x) & 1) * 2 + ((root ^ k) & 1),
         ((root >> 4) ^ (x // 2)) & 1,
         ((root >> 1) ^ y) & 1,
         ((root >> 2) ^ (y // 2)) & 1,
     )
+    opposite = x + 1 - 2 * (x % 2)
     reg_targets = (
         partner,
-        device(x + 1 - 2 * (x % 2), y, k),
+        device(opposite, y, k),
+        device(opposite, y, 1 - k),
         device(SIDE - 1 - x, y, k),
         device(x, y + 1 - 2 * (y % 2), k),
         device(x, SIDE - 1 - y, k),
@@ -290,10 +315,10 @@
     )
 
     def reg_copy(i):
-        if i == 0:
-            src, dst = regs_in.at[1 - k], regs_pair[0].at[1]
-        elif i < 5:
-            src, dst = regs_pair[i].at[0], regs_pair[i].at[1]
+        if i < 3:
+            src, dst = regs_in.at[k if i == 1 else 1 - k], regs_pair[0].at[i + 1]
+        elif i < REG_COPIES - 1:
+            src, dst = regs_pair[i - 2].at[0], regs_pair[i - 2].at[1]
         else:
             src, dst = regs.at[k], regs.at[k]
         return remote(src, dst, reg_send.at[i], reg_recv.at[i], reg_targets[i])
@@ -302,22 +327,22 @@
         if i == 0:
             for c in range(2):
                 load_regs(c).wait()
+            for n in range(3):
+                reg_copy(n).start()
             regs_pair[0][0] = regs_in[k]
+            return
+        for n in range(3) if i == 1 else (i + 1,):
+            reg_copy(n).wait_recv()
+        chosen = regs_pair[i - 1][sides[i - 1]]
+        if i < REG_STEPS - 1:
+            regs_pair[i][0] = chosen
         else:
-            reg_copy(i - 1).wait_recv()
-            chosen = pair_of(i - 1)
-            if i < 5:
-                regs_pair[i][0] = chosen
-            else:
-                regs[k] = chosen
-        reg_copy(i).start()
-
-    def pair_of(i):
-        return regs_pair[i][sides[i]]
+            regs[k] = chosen
+        reg_copy(i + 2).start()
 
     def regs_here():
         remote(
-            regs.at[1 - k], regs.at[1 - k], reg_send.at[5], reg_recv.at[5], partner
+            regs.at[1 - k], regs.at[1 - k], reg_send.at[REG_COPIES - 1], reg_recv.at[REG_COPIES - 1], partner
         ).wait_recv()
 
     def give(u, f):
@@ -367,17 +392,10 @@
             give(u, 5)
 
     def all_here(u):
-        h = u // 2
-        for core in range(CORES):
-            for i in range(LEAVES):
-                ref = received[u].at[slot(core, LEAF[i][0])]
-                remote(
-                    ref, ref, leaf_send.at[u, 0], leaf_recv.at[u, core * LEAVES + i], partner
-                ).wait_recv()
-        for f in range(PLACES):
-            ref = received[u].at[slot(1 - k, FULL[f][0])]
-            remote(ref, ref, pair_send.at[u, f], pair_recv.at[u, f], partner).wait_recv()
-        if u % 2 == 0:
+        h, c = ORDER[u]
+        ref = received[u].at[pl.ds(0, MESSAGES)]
+        remote(ref, ref, unit_send.at[u], unit_recv.at[u], partner).wait_recv()
+        if c == 0:
             load_q(h).wait()
             spare = regs[0, :, pl.ds(h * HEAD_SIZE, HEAD_SIZE)]
             received[u][slot(k, (0, 0))] = jnp.concatenate([spare, spare], axis=0)
@@ -406,16 +424,16 @@
 
     def keys_of(h, b, places):
         return key_pairs(
-            full_refs[2 * h][0][b],
+            full_refs[KEYS[h]][0][b],
             regs[0, :, pl.ds(h * HEAD_SIZE, HEAD_SIZE)],
-            [received[2 * h][place] for place, _ in places],
+            [received[KEYS[h]][place] for place, _ in places],
         )
 
     def values_of(h, b, places):
         return value_pairs(
-            full_refs[2 * h + 1][0][b],
+            full_refs[VALUES[h]][0][b],
             regs[1, :, pl.ds(h * HEAD_SIZE, HEAD_SIZE)],
-            [received[2 * h + 1][place] for place, _ in places],
+            [received[VALUES[h]][place] for place, _ in places],
             [marks[used] for _, used in places],
         )
 
@@ -424,24 +442,6 @@
         return stacked_heads(q_here[here, pl.ds(h * width, width)])
 
     part = rows * GROUP // PARTS
-
-    def compute(h, start, stop):
-        @pl.loop(start, stop)
-        def _(b):
-            places = far_slots(b)
-            stacked = queries_of(h, b)
-            keys, values = keys_of(h, b, places), values_of(h, b, places)
-            seen = seen_rows(rows, image[b])
-            scores = [score(stacked, keys, seen, 0, part)]
-            outs = []
-            for n in range(PARTS):
-                if n + 1 < PARTS:
-                    scores.append(
-                        score(stacked, keys, seen, (n + 1) * part, (n + 2) * part)
-                    )
-                outs.append(finish(soften(scores[n]), values))
-            out_here[h * blocks + b] = spread_heads(jnp.concatenate(outs, axis=0), rows)
-            store(h, b).start()
 
     def compute_weights(h):
         @pl.loop(0, blocks)
@@ -456,69 +456,56 @@
                         score(stacked, keys, seen, (n + 1) * part, (n + 2) * part)
                     )
                 for i, w in enumerate(soften(scores[n])):
-                    weights_here[b, i, pl.ds(n * part, part)] = w
+                    weights_here[h % 2, b, i, pl.ds(n * part, part)] = w
 
     def compute_outputs(h):
         @pl.loop(0, blocks)
         def _(b):
             values = values_of(h, b, far_slots(b))
             pairs = len(values)
-            outs = finish([weights_here[b, i] for i in range(pairs)], values)
+            outs = finish([weights_here[h % 2, b, i] for i in range(pairs)], values)
             out_here[h * blocks + b] = spread_heads(outs, rows)
             store(h, b).start()
 
-    begin(0)
-    begin(1)
     reg_step(0)
-    begin(2)
-    for i in range(PARTNER + 1):
-        ref = asks.at[i]
-        remote(ref, ref, ask_send.at[i], ask_recv.at[i], partner).wait_recv()
+    for u in range(LEAD):
+        begin(u)
+    others = asks.at[pl.ds(0, SELF)]
+    remote(others, others, ask_send.at[0], ask_recv.at[0], partner).wait_recv()
     to_scalars = pltpu.make_async_copy(asks, asks_s, table_sem.at[0])
     to_scalars.start()
     to_scalars.wait()
     stage(0, 0)
-    stage(1, 0)
     reg_step(1)
-    stage(2, 0)
-    last = KEY_VALUE_HEADS - 1
-    half = blocks // 2
-    for t in range(UNITS + 2):
+    for u in range(1, LEAD):
+        stage(u, 0)
+    for t in range(UNITS + 3):
         stage(t, 1)
         stage(t - 1, 2)
         stage(t - 2, 3)
-        if t + 3 < UNITS:
-            begin(t + 3)
-            stage(t + 3, 0)
+        if t + LEAD < UNITS:
+            begin(t + LEAD)
+            stage(t + LEAD, 0)
         if t + 2 < REG_STEPS:
             reg_step(t + 2)
-        if t == REG_STEPS - 2:
+        elif t + 2 == REG_STEPS:
             regs_here()
-        if t >= 4:
-            h = t // 2 - 2
-            if t % 2 == 0:
-                all_here(2 * h)
-                all_here(2 * h + 1)
-                compute(h, 0, half)
+        if t >= 3:
+            h, c = ORDER[t - 3]
+            all_here(t - 3)
+            if c == 0:
+                compute_weights(h)
             else:
-                compute(h, half, blocks)
-    all_here(2 * last)
-    compute_weights(last)
-    all_here(2 * last + 1)
-    compute_outputs(last)
-
-    for i in range(PARTNER + 1):
-        ask(i).wait_send()
-    for i in range(REG_STEPS):
+                compute_outputs(h)
+
+    remote(others, others, ask_send.at[0], ask_recv.at[0], partner).wait_send()
+    for i in range(REG_COPIES):
         reg_copy(i).wait_send()
     for u in range(UNITS):
-        for f in range(1, PLACES):
-            full(u, f).wait_send()
-        for f in range(PLACES):
-            across(u, f).wait_send()
-        for i in range(LEAVES):
-            for core in range(CORES):
-                leaf(u, i, core).wait_send()
+        sent = outgoing.at[u]
+        remote(sent, sent, unit_send.at[u], unit_recv.at[u], partner).wait_send()
+        sent = outgoing.at[u, pl.ds(0, (PLACES - 1) * blocks)]
+        remote(sent, sent, full_send.at[u], unit_recv.at[u], partner).wait_send()
     for h in range(KEY_VALUE_HEADS):
         for b in range(blocks):
             store(h, b).wait()
@@ -535,12 +522,14 @@
     return pl.pallas_call(
         layer_kernel,
         out_shape=jax.ShapeDtypeStruct(q.shape, bf16),
-        in_specs=[pl.BlockSpec(memory_space=pl.ANY)] * 3
-        + [pl.BlockSpec(memory_space=pltpu.SMEM)] * 4,
+        in_specs=[pl.BlockSpec(memory_space=pl.ANY)] * 7,
         out_specs=pl.BlockSpec(memory_space=pl.ANY),
-        scratch_shapes=[pltpu.VMEM((blocks, rows, HEAD_SIZE), bf16)] * (UNITS * PLACES)
+        scratch_shapes=[pltpu.SMEM(a.shape, jnp.int32) for a in (lists, counts, image, owner)]
+        + [dma((4,))]
+        + [pltpu.VMEM((blocks, rows, HEAD_SIZE), bf16)] * (UNITS * PLACES)
         + [pltpu.VMEM((CORES * CHIP_SLOTS, rows, HEAD_SIZE), bf16)] * UNITS
-        + [pltpu.VMEM((2, REG, kv_width), bf16)] * (REG_STEPS - 1)
+        + [pltpu.VMEM((4, REG, kv_width), bf16)]
+        + [pltpu.VMEM((2, REG, kv_width), bf16)] * (REG_STEPS - 2)
         + [
             pltpu.VMEM((UNITS, 2 * LEAVES + PLACES, rows, HEAD_SIZE), bf16),
             pltpu.VMEM((ASKERS, 1, 128), jnp.int32),
@@ -550,22 +539,20 @@
             pltpu.VMEM((2, REG, kv_width), bf16),
             pltpu.VMEM(q.shape, bf16),
             pltpu.VMEM((heads * blocks, rows, width), bf16),
-            pltpu.VMEM((blocks, (slots + 2) // 2, GROUP * rows, 2 * rows), bf16),
+            pltpu.VMEM((2, blocks, (slots + 2) // 2, GROUP * rows, 2 * rows), bf16),
             dma((1,)),
             dma((UNITS,)),
             dma((2,)),
             dma((heads,)),
             dma((heads * blocks,)),
-            dma((PARTNER + 1,)),
-            dma((PARTNER + 1,)),
-            dma((REG_STEPS,)),
-            dma((REG_STEPS,)),
+            dma((1,)),
+            dma((1,)),
+            dma((REG_COPIES,)),
+            dma((REG_COPIES,)),
+            dma((UNITS,)),
             dma((UNITS, PLACES)),
-            dma((UNITS, PLACES)),
-            dma((UNITS, 2 * LEAVES)),
-            dma((UNITS, 2 * LEAVES)),
-            dma((UNITS, PLACES)),
-            dma((UNITS, PLACES)),
+            dma((UNITS,)),
+            dma((UNITS,)),
         ],
         compiler_params=pltpu.CompilerParams(
             collective_id=0, has_side_effects=True, vmem_limit_bytes=62 << 20

time: 90.9 us -> 82.4 us (0.906)
  Pallas kernels: 86 us -> 77.5 us
    pallas_call x1, Pallas kernels: 86 us -> 77.5 us  [layer(): pl.pallas_call(layer_kernel, out_shape=jax.ShapeDtypeStruct(q.shape, bf16...]
where the time goes in v4:
time: 82.4 us; the launch traced here: 82.3 us
  Pallas kernels  77.5 us (94%)
  local copies, waits for them, and re-layouts  4.11 us (5%)
    pallas_call x1, Pallas kernels, layer(): pl.pallas_call(layer_kernel, out_shape=jax.ShapeDtypeStruct(q.shape, bf16...  77.5 us
    unnamed x1, local copies, waits for them, and re-layouts  4.11 us

profile of v4, /device:TPU:1, one launch (start us, length us, event | category | flops | bytes accessed | tf_op | source)
XLA Modules:
  0.0 82.3 jit_solution(10813602637091600099)
XLA Ops:
  0.7 77.5 %layer.1 = bf16[512,3584]{1,0:T(8,128)(2,1)} custom-call(bf16[512,3584]{1,0:T(8,128)(2,1)} %bitcast.8, bf16[4,128,512]{2,1,0:T(8,128)(2,1)} %bitcast.9, bf16[4,128,512]{2,1,0:T(8,128)(2,1)} %bitcast.10, s32[4,8]{1,0:T(4,128)} %bitcast.11, s32[4]{0:T(128)} %bitcast.12, s32[4]{0:T(128)} %bitcast.13, s32[1]{0:T(128)S(6)} %copy.9.owner_hbm), custom_call_target="tpu_custom_call" | custom-call | tf_op jit(solution)/shard_map/layer/pallas_call | solution.py:522
  78.2 4.1 %copy.10 = bf16[1,512,3584]{2,1,0:T(8,128)(2,1)} copy(bf16[1,512,3584]{2,1,0:T(8,128)(2,1)} %bitcast.7) | data formatting | bytes 7340032

commit v5 on v4

--- a/solution.py
+++ b/solution.py
@@ -467,8 +467,9 @@
             out_here[h * blocks + b] = spread_heads(outs, rows)
             store(h, b).start()
 
+    begin(0)
     reg_step(0)
-    for u in range(LEAD):
+    for u in range(1, LEAD):
         begin(u)
     others = asks.at[pl.ds(0, SELF)]
     remote(others, others, ask_send.at[0], ask_recv.at[0], partner).wait_recv()

time: 82.4 us -> 83.9 us (1.018)
  Pallas kernels: 77.5 us -> 79 us
    pallas_call x1, Pallas kernels: 77.5 us -> 79 us  [layer(): pl.pallas_call(layer_kernel, out_shape=jax.ShapeDtypeStruct(q.shape, bf16...]
where the time goes in v5:
time: 83.9 us; the launch traced here: 83.8 us
  Pallas kernels  79 us (94%)
  local copies, waits for them, and re-layouts  4.11 us (5%)
    pallas_call x1, Pallas kernels, layer(): pl.pallas_call(layer_kernel, out_shape=jax.ShapeDtypeStruct(q.shape, bf16...  79 us
    unnamed x1, local copies, waits for them, and re-layouts  4.11 us

profile of v5, /device:TPU:1, one launch (start us, length us, event | category | flops | bytes accessed | tf_op | source)
XLA Modules:
  0.0 83.8 jit_solution(9886369119075219936)
XLA Ops:
  0.7 79.0 %layer.1 = bf16[512,3584]{1,0:T(8,128)(2,1)} custom-call(bf16[512,3584]{1,0:T(8,128)(2,1)} %bitcast.8, bf16[4,128,512]{2,1,0:T(8,128)(2,1)} %bitcast.9, bf16[4,128,512]{2,1,0:T(8,128)(2,1)} %bitcast.10, s32[4,8]{1,0:T(4,128)} %bitcast.11, s32[4]{0:T(128)} %bitcast.12, s32[4]{0:T(128)} %bitcast.13, s32[1]{0:T(128)S(6)} %copy.9.owner_hbm), custom_call_target="tpu_custom_call" | custom-call | tf_op jit(solution)/shard_map/layer/pallas_call | solution.py:523
  79.7 4.1 %copy.10 = bf16[1,512,3584]{2,1,0:T(8,128)(2,1)} copy(bf16[1,512,3584]{2,1,0:T(8,128)(2,1)} %bitcast.7) | data formatting | bytes 7340032
